TPU v7x, 256 devices: a whole 4x4x8 slice. The times are simulated.
256 devices in a mesh: dp: 16 (over y, x), shard: 16 (over z, core).
Axes of the slice: x: 4, y: 4, z: 8, core: 2. Of those that a mesh axis runs over, the one named last changes fastest.
Arguments:
- gradients: bfloat16 [16, 12288, 2048], P('dp', 'shard'), may hold values from -4000 to 4000, as said below
- master_weights: float32 [12288, 2048], P(('shard', 'dp')), may hold values from -6 to 6
- first_moment: float32 [12288, 2048], P(('shard', 'dp')), may hold values from -4 to 4
- second_moment: float32 [12288, 2048], P(('shard', 'dp')), may hold values from 0.05 to 2
Outputs:
- parameters: bfloat16 [12288, 2048], P('shard')
- new_master: float32 [12288, 2048], P(('shard', 'dp'))
- new_first: float32 [12288, 2048], P(('shard', 'dp'))
- new_second: float32 [12288, 2048], P(('shard', 'dp'))
Inputs may be any that keep to these rules, and one draw needn't show every extreme that they name: `gradients`: each replica's partial gradient.
All inputs are finite; a program needn't handle non-finite values.
Results may differ from a plain program's by a relative error of at most 0.006.
Values may be sent and summed in bfloat16 or wider, within the bound.
No kernel may reach another device: no remote copies, remote signals or barrier semaphores. Data moves between devices by JAX's collectives and lax.ppermute only.
A program may use at most 64 MiB of HBM per device.

v0:
```python
import math

import jax
import jax.numpy as jnp
from jax import lax
from jax.sharding import Mesh
from jax.sharding import PartitionSpec as P

DP = ("dp_0", "dp_1")
SHARD = ("shard_0", "shard_1")
SHARD_DP = ("shard_0", "shard_1", "dp_0", "dp_1")


first_bias = 1.0 - math.exp(100.0 * math.log(0.9))
second_bias = 1.0 - math.exp(100.0 * math.log(0.95))


def split_up(array, dim, size):
    lengths = array.shape
    pieces = array.reshape(*lengths[:dim], size, lengths[dim] // size, *lengths[dim + 1 :])
    return jnp.moveaxis(pieces, dim, 0)


def sent_and_summed(array, axis, dim):
    pieces = split_up(array, dim, lax.axis_size(axis))
    arrived = lax.all_to_all(pieces, axis, split_axis=0, concat_axis=0, tiled=True)
    return arrived.astype(jnp.float32).sum(axis=0)


def sent_to_all(array, axis):
    size = lax.axis_size(axis)
    return lax.all_to_all(
        jnp.broadcast_to(array[None], (size, *array.shape)), axis, 0, 0, tiled=True
    )


def of_everyone(array, axis):
    everything = sent_to_all(array, axis)
    return jnp.sum(everything, axis=0)


def one_axis_at_a_time(array, axes):
    far, near = axes
    nearer = of_everyone(array, near)
    return of_everyone(nearer, far)


def in_order(pieces, dim):
    lengths = list(pieces.shape[1:])
    lengths[dim] *= pieces.shape[0]
    return jnp.moveaxis(pieces, 0, dim).reshape(lengths)


def gathered_copies(array, axis, dim):
    pieces = sent_to_all(array, axis)
    return in_order(pieces, dim)


def adam_update(summed, factor, master_weights, first_moment, second_moment):
    clipped = factor * summed
    new_first = 0.9 * first_moment + 0.1 * clipped
    new_second = 0.95 * second_moment + 0.05 * clipped * clipped
    first_hat = new_first / first_bias
    second_hat = new_second / second_bias
    new_master = master_weights - 0.01 * (
        first_hat / (jnp.sqrt(second_hat) + 1e-08) + 0.1 * master_weights
    )
    return (new_master, new_first, new_second)


def per_device(gradients, master_weights, first_moment, second_moment):
    rows_dev = master_weights.shape[0]
    width = master_weights.shape[1]
    entries = rows_dev * lax.axis_size(DP) * lax.axis_size(SHARD) * width
    local_grad = gradients[0].astype(jnp.float32)
    summed = sent_and_summed(local_grad.astype(jnp.bfloat16), DP, 0)
    square_sum = one_axis_at_a_time(
        jnp.sum(summed * summed), ("dp_0", ("dp_1", "shard_0", "shard_1"))
    )
    limit = 0.5 * math.sqrt(entries)
    factor = jnp.minimum(1.0, limit / jnp.sqrt(square_sum + 1e-06))
    new_master, new_first, new_second = adam_update(
        summed, factor, master_weights, first_moment, second_moment
    )
    owned_params = new_master.astype(jnp.bfloat16)
    parameters = gathered_copies(owned_params, DP, 0)
    return (parameters, new_master, new_first, new_second)


def solution(mesh):
    split = Mesh(mesh.devices.reshape(4, 4, 8, 2), ("dp_0", "dp_1", "shard_0", "shard_1"))
    return jax.shard_map(
        per_device,
        mesh=split,
        in_specs=(P(DP, SHARD, None), P(SHARD_DP, None), P(SHARD_DP, None), P(SHARD_DP, None)),
        out_specs=(P(SHARD, None), P(SHARD_DP, None), P(SHARD_DP, None), P(SHARD_DP, None)),
        check_vma=False,
    )
```

profile of v0, /device:TPU:2, one launch (start us, length us, event | category | flops | bytes accessed | tf_op | source)
XLA Modules:
  0.0 124.5 jit_solution(8021457390038427170)
XLA Ops:
  0.6 45.7 %all_to_all.22 = bf16[16,48,2048]{2,1,0:T(8,128)(2,1)S(1)} all-to-all(bf16[16,48,2048]{2,1,0:T(8,128)(2,1)} %bitcast.3), channel_id=1, replica_groups=mesh['dp_0'=4,'dp_1'=4,'shard_0'=8,'shard_1'=2] {'dp_0','dp_1'}, dimensions={0} | all-to-all | bytes 6291456 | tf_op jit(solution)/shard_map/all_to_all | solution.py:26
  46.4 0.0 copy-start
  46.4 0.0 copy-start.1
  46.4 0.0 copy-start.2
  46.4 0.6 convert_reduce_fusion
  47.0 0.7 multiply_reduce_fusion
  47.7 0.7 broadcast_in_dim.6
  48.4 19.2 %all_to_all.23 = f32[64,1,1]{2,1,0:T(1,128)S(1)} all-to-all(f32[64,1,1]{2,1,0:T(1,128)S(1)} %broadcast_in_dim.6), channel_id=1, replica_groups=mesh['dp_0'=4,'dp_1'=4,'shard_0'=8,'shard_1'=2] {'dp_1','shard_0','shard..., dimensions={0} | all-to-all | bytes 512 | tf_op jit(solution)/shard_map/all_to_all | solution.py:32
  67.5 0.7 reduce_sum.38
  68.2 0.6 broadcast_in_dim.7
  68.8 7.9 %all_to_all.24 = f32[4,1,1]{2,1,0:T(1,128)S(1)} all-to-all(f32[4,1,1]{2,1,0:T(1,128)S(1)} %broadcast_in_dim.7), channel_id=1, replica_groups=mesh['dp_0'=4,'dp_1'=4,'shard_0'=8,'shard_1'=2] {'dp_0'}, dimensions={0} | all-to-all | bytes 32 | tf_op jit(solution)/shard_map/all_to_all | solution.py:32
  76.7 0.6 reduce_sum.39
  78.0 0.0 copy-done
  78.0 0.0 copy-done.1
  78.0 0.0 copy-done.2
  78.0 1.2 fusion.1
  79.2 0.4 broadcast_in_dim.8
  79.6 43.2 %all_to_all.25 = bf16[16,48,2048]{2,1,0:T(8,128)(2,1)S(1)} all-to-all(bf16[16,48,2048]{2,1,0:T(8,128)(2,1)S(1)} %broadcast_in_dim.8), channel_id=1, replica_groups=mesh['dp_0'=4,'dp_1'=4,'shard_0'=8,'shard_1'=2] {'dp_0','dp_1'}, dimensions={0} | all-to-all | bytes 6291456 | tf_op jit(solution)/shard_map/all_to_all | solution.py:32
  122.8 1.7 %copy.13 = bf16[768,2048]{1,0:T(8,128)(2,1)} copy(bf16[768,2048]{1,0:T(8,128)(2,1)S(1)} %bitcast.2) | data formatting | bytes 6291456
Async XLA Ops:
  46.4 31.6 %copy-start = (f32[48,2048]{1,0:T(8,128)S(1)}, f32[48,2048]{1,0:T(8,128)}, u32[]{:S(2)}) copy-start(f32[48,2048]{1,0:T(8,128)} %param.5) | copy-start | bytes 1179652
  46.4 31.6 %copy-start.1 = (f32[48,2048]{1,0:T(8,128)S(1)}, f32[48,2048]{1,0:T(8,128)}, u32[]{:S(2)}) copy-start(f32[48,2048]{1,0:T(8,128)} %param.6) | copy-start | bytes 1179652
  46.4 31.7 %copy-start.2 = (f32[48,2048]{1,0:T(8,128)S(1)}, f32[48,2048]{1,0:T(8,128)}, u32[]{:S(2)}) copy-start(f32[48,2048]{1,0:T(8,128)} %param.7) | copy-start | bytes 1179652
where the time goes:
time: 125 us
  blocking collectives  116 us (93%)
  other arithmetic  3.77 us (3%)
  local copies, waits for them, and re-layouts  3.36 us (3%)
  between operations  1.38 us (1%)
    all_to_all x3, blocking collectives, sent_to_all(): lax.all_to_all(jnp.broadcast_to(array[None], (size, *array.shape)), axis,...  70.3 us
    all_to_all x1, blocking collectives, sent_and_summed(): lax.all_to_all(pieces, axis, split_axis=0, concat_axis=0, tiled=True)  45.7 us

commit v1 on v0

v1 whole, which is shorter than its diff:
```python
import math

import jax
import jax.numpy as jnp
from jax import lax
from jax.experimental import pallas as pl
from jax.experimental.pallas import tpu as pltpu
from jax.sharding import Mesh
from jax.sharding import PartitionSpec as P

DP = ("dp_0", "dp_1")
SHARD = ("shard_0", "shard_1")
SHARD_DP = ("shard_0", "shard_1", "dp_0", "dp_1")
PAIRED = ("dp_0", "dp_1", "shard_1")
SIDE = 4


first_bias = 1.0 - math.exp(100.0 * math.log(0.9))
second_bias = 1.0 - math.exp(100.0 * math.log(0.95))


def moved(array, axis, by):
    pairs = []
    for y in range(SIDE):
        for x in range(SIDE):
            for core in range(2):
                to_y, to_x = (y, (x + by) % SIDE) if axis == core else ((y + by) % SIDE, x)
                pairs.append(((y * SIDE + x) * 2 + core, (to_y * SIDE + to_x) * 2 + core))
    return lax.ppermute(array, PAIRED, pairs)


def block_at(first, second):
    y, x, core = (lax.axis_index(name) for name in ("dp_0", "dp_1", "shard_1"))
    off_x = jnp.where(core == 0, first, second)
    off_y = jnp.where(core == 0, second, first)
    return lax.rem(y + off_y, SIDE) * SIDE + lax.rem(x + off_x, SIDE)


def picked(gradients, first, seconds, rows):
    width = gradients.shape[-1]

    def kernel(source, target, sems):
        copies = []
        for i, second in enumerate(seconds):
            at = pl.multiple_of(block_at(first, second) * rows, rows)
            copy = pltpu.make_async_copy(
                source.at[0, pl.ds(at, rows)], target.at[pl.ds(i * rows, rows)], sems.at[i]
            )
            copy.start()
            copies.append(copy)
        for copy in copies:
            copy.wait()

    count = len(seconds)
    return pl.pallas_call(
        kernel,
        out_shape=jax.ShapeDtypeStruct((count * rows, width), gradients.dtype),
        in_specs=[pl.BlockSpec(memory_space=pltpu.HBM)],
        out_specs=pl.BlockSpec(memory_space=pl.ANY),
        scratch_shapes=[pltpu.SemaphoreType.DMA((count,))],
        compiler_params=pltpu.CompilerParams(vmem_limit_bytes=1 << 20),
        cost_estimate=pl.CostEstimate(
            flops=2000000, bytes_accessed=4 * count * rows * width, transcendentals=0
        ),
    )(gradients)


def placed(pieces, places, rows, whole):
    width = pieces[0].shape[-1]
    count = sum(len(p) for p in places)

    def kernel(*refs):
        target, sems = refs[-2:]
        copies = []
        for source, own_places in zip(refs, places):
            for i, (first, second) in enumerate(own_places):
                at = pl.multiple_of(block_at(first, second) * rows, rows)
                copy = pltpu.make_async_copy(
                    source.at[pl.ds(i * rows, rows)],
                    target.at[pl.ds(at, rows)],
                    sems.at[len(copies)],
                )
                copy.start()
                copies.append(copy)
        for copy in copies:
            copy.wait()

    more = () if whole is None else (whole,)
    return pl.pallas_call(
        kernel,
        out_shape=jax.ShapeDtypeStruct((SIDE * SIDE * rows, width), pieces[0].dtype),
        in_specs=[pl.BlockSpec(memory_space=pl.ANY)] * (len(pieces) + len(more)),
        out_specs=pl.BlockSpec(memory_space=pl.ANY),
        scratch_shapes=[pltpu.SemaphoreType.DMA((count,))],
        input_output_aliases={len(pieces): 0} if more else {},
        compiler_params=pltpu.CompilerParams(vmem_limit_bytes=1 << 20),
        cost_estimate=pl.CostEstimate(
            flops=2000000, bytes_accessed=4 * count * rows * width, transcendentals=0
        ),
    )(*pieces, *more)


def of_everyone(partial, axes):
    size = lax.axis_size(axes)
    sent = jnp.broadcast_to(partial[None], (size, *partial.shape))
    return lax.all_to_all(sent, axes, 0, 0, tiled=True)


def adam_update(summed, factor, master_weights, first_moment, second_moment):
    clipped = factor * summed
    new_first = 0.9 * first_moment + 0.1 * clipped
    new_second = 0.95 * second_moment + 0.05 * clipped * clipped
    first_hat = new_first / first_bias
    second_hat = new_second / second_bias
    new_master = master_weights - 0.01 * (
        first_hat / (jnp.sqrt(second_hat) + 1e-08) + 0.1 * master_weights
    )
    return (new_master, new_first, new_second)


def reduced(gradients, rows):
    f32 = jnp.float32
    onward = range(1, SIDE)
    passing = {}
    for d in (2, 1, 3):
        passing[d] = moved(picked(gradients, d, onward, rows), 0, d).astype(f32)
    staying = {}
    for d in (2, 1, 3):
        staying[d] = moved(picked(gradients, d, (0,), rows), 0, d).astype(f32)
    total = picked(gradients, 0, onward, rows).astype(f32) + sum(passing.values())
    arrived = {}
    for e in (2, 1, 3):
        piece = total[(e - 1) * rows : e * rows].astype(jnp.bfloat16)
        arrived[e] = moved(piece, 1, e).astype(f32)
    own = picked(gradients, 0, (0,), rows).astype(f32) + sum(staying.values())
    return own + sum(arrived.values())


def gathered(owned, rows):
    nearby = {e: moved(owned, 1, e) for e in (2, 1, 3)}
    along = {d: moved(owned, 0, d) for d in (2, 1, 3)}
    held = jnp.concatenate([nearby[e] for e in (1, 2, 3)])
    rest = {d: moved(held, 0, d) for d in (2, 1, 3)}
    early = [owned] + [nearby[e] for e in (1, 2, 3)] + [along[d] for d in (1, 2, 3)]
    places = [[(0, 0)]] + [[(0, -e)] for e in (1, 2, 3)] + [[(-d, 0)] for d in (1, 2, 3)]
    places = [[(f % SIDE, s % SIDE) for f, s in p] for p in places]
    out = placed(early, places, rows, None)
    late = [rest[d] for d in (1, 2, 3)]
    places = [[(-d % SIDE, -e % SIDE) for e in (1, 2, 3)] for d in (1, 2, 3)]
    return placed(late, places, rows, out)


def step(gradients, master_weights, first_moment, second_moment):
    rows, width = master_weights.shape
    entries = rows * lax.axis_size(DP) * lax.axis_size(SHARD) * width
    summed = reduced(gradients, rows)
    partial = jnp.sum(jnp.sum(summed * summed, axis=0).reshape(16, width // 16), axis=0)
    partial = jnp.sum(of_everyone(partial[None], SHARD), axis=0)
    square_sum = jnp.sum(of_everyone(partial, DP), axis=(0, 2))[:, None]
    limit = 0.5 * math.sqrt(entries)
    factor = jnp.minimum(1.0, limit / jnp.sqrt(square_sum + 1e-06))
    new_master, new_first, new_second = adam_update(
        summed, factor, master_weights, first_moment, second_moment
    )
    parameters = gathered(new_master.astype(jnp.bfloat16), rows)
    return (parameters, new_master, new_first, new_second)


def solution(mesh):
    split = Mesh(mesh.devices.reshape(4, 4, 8, 2), ("dp_0", "dp_1", "shard_0", "shard_1"))
    return jax.shard_map(
        step,
        mesh=split,
        in_specs=(P(DP, SHARD, None), P(SHARD_DP, None), P(SHARD_DP, None), P(SHARD_DP, None)),
        out_specs=(P(SHARD, None), P(SHARD_DP, None), P(SHARD_DP, None), P(SHARD_DP, None)),
        check_vma=False,
    )
```

time: 125 us -> 105 us (0.84)
  blocking collectives: 116 us -> 28.8 us
  starting transfers between devices: 0 us -> 32.5 us
  waiting for transfers between devices: 0 us -> 29.7 us
  Pallas kernels: 0 us -> 6.49 us
  local copies, waits for them, and re-layouts: 3.36 us -> 2.01 us
  other arithmetic: 3.77 us -> 2.45 us
    all_to_all x4 -> x2, blocking collectives: 116 us -> 28.8 us  [of_everyone(): return lax.all_to_all(sent, axes, 0, 0, tiled=True)]
    ppermute x0 -> x18, starting transfers between devices: none -> 32.5 us  [moved(): return lax.ppermute(array, PAIRED, pairs)]
    ppermute x0 -> x18, waiting for transfers between devices: none -> 29.7 us  [moved(): return lax.ppermute(array, PAIRED, pairs)]
    pallas_call x0 -> x10, Pallas kernels: none -> 6.49 us  [the longest x8 4.07 us: picked(): pl.pallas_call(kernel, out_shape=jax.ShapeDtypeStruct((count * rows, widt...]
    reduce_sum x4, other arithmetic: 2.57 us -> 0.85 us  [the longest x1 0.6 us: step(): square_sum = jnp.sum(of_everyone(partial, DP), axis=(0, 2))[:, None]]
    broadcast_in_dim x3 -> x2, local copies, waits for them, and re-layouts: 1.68 us -> 0.02 us  [of_everyone(): sent = jnp.broadcast_to(partial[None], (size, *partial.shape))]
  transfers between devices with their start and end apart: 0 -> 18, of which waited for: 0 -> 8; matrix products, arithmetic and copies ran while one was open for 0% -> 0% of each run, Pallas kernels for 0% -> 4%
where the time goes in v1:
time: 105 us; the launch traced here: 104 us
  starting transfers between devices  32.5 us (31%)
  waiting for transfers between devices  29.7 us (28%)
  blocking collectives  28.8 us (27%)
  Pallas kernels  6.49 us (6%)
  other arithmetic  2.45 us (2%)
  local copies, waits for them, and re-layouts  2.01 us (2%)
  between operations  1.55 us (1%)
    ppermute x18, starting transfers between devices, moved(): return lax.ppermute(array, PAIRED, pairs)  32.5 us
    ppermute x18, waiting for transfers between devices, moved(): return lax.ppermute(array, PAIRED, pairs)  29.7 us
    all_to_all x2, blocking collectives, of_everyone(): return lax.all_to_all(sent, axes, 0, 0, tiled=True)  28.8 us
    pallas_call x8, Pallas kernels, picked(): pl.pallas_call(kernel, out_shape=jax.ShapeDtypeStruct((count * rows, widt...  4.07 us
    pallas_call x2, Pallas kernels, placed(): pl.pallas_call(kernel, out_shape=jax.ShapeDtypeStruct((SIDE * SIDE * rows...  2.41 us
  transfers between devices with their start and end apart: 18, of which 8 were waited for; matrix products, arithmetic and copies ran while one was open for 0% of the time, Pallas kernels for 4%

profile of v1, /device:TPU:2, one launch (start us, length us, event | category | flops | bytes accessed | tf_op | source)
XLA Modules:
  0.0 103.6 jit_solution(12364057407034876721)
XLA Ops:
  0.6 1.9 %copy-done = bf16[1,768,2048]{2,1,0:T(8,128)(2,1)S(1)} copy-done((bf16[1,768,2048]{2,1,0:T(8,128)(2,1)S(1)}, bf16[1,768,2048]{2,1,0:T(8,128)(2,1)}, u32[]{:S(2)}) %copy-start) | copy-done | bytes 3145752
  2.5 0.8 shard_map.81
  3.3 1.6 %collective-permute-start.4 = (bf16[144,2048]{1,0:T(8,128)(2,1)S(1)}, bf16[144,2048]{1,0:T(8,128)(2,1)S(1)}, u32[]{:S(2)}, u32[]{:S(2)}) collective-permute-start(bf16[144,2048]{1,0:T(8,128)(2,1)S(1)} %shard_map.81), channel_id=1, source_target_pairs={{0,16},{1,65},{16,32},{17,81},{32,48},{33,97},{48,0},{49,113},{64,... | collective-permute-start | bytes 1769480 | tf_op jit(solution)/shard_map/ppermute | solution.py:29
  4.9 0.8 shard_map.82
  5.7 1.8 %collective-permute-start.5 = (bf16[144,2048]{1,0:T(8,128)(2,1)S(1)}, bf16[144,2048]{1,0:T(8,128)(2,1)S(1)}, u32[]{:S(2)}, u32[]{:S(2)}) collective-permute-start(bf16[144,2048]{1,0:T(8,128)(2,1)S(1)} %shard_map.82), channel_id=1, source_target_pairs={{0,48},{1,193},{16,0},{17,209},{32,16},{33,225},{48,32},{49,241},{... | collective-permute-start | bytes 1769480 | tf_op jit(solution)/shard_map/ppermute | solution.py:29
  7.5 0.8 shard_map.80
  8.3 1.2 %collective-permute-start.3 = (bf16[144,2048]{1,0:T(8,128)(2,1)S(1)}, bf16[144,2048]{1,0:T(8,128)(2,1)S(1)}, u32[]{:S(2)}, u32[]{:S(2)}) collective-permute-start(bf16[144,2048]{1,0:T(8,128)(2,1)S(1)} %shard_map.80), channel_id=1, source_target_pairs={{0,32},{1,129},{16,48},{17,145},{32,0},{33,161},{48,16},{49,177},{... | collective-permute-start | bytes 1769480 | tf_op jit(solution)/shard_map/ppermute | solution.py:29
  9.5 0.2 shard_map.76
  9.7 2.5 %collective-permute-start = (bf16[48,2048]{1,0:T(8,128)(2,1)S(1)}, bf16[48,2048]{1,0:T(8,128)(2,1)S(1)}, u32[]{:S(2)}, u32[]{:S(2)}) collective-permute-start(bf16[48,2048]{1,0:T(8,128)(2,1)S(1)} %shard_map.76), channel_id=1, source_target_pairs={{0,32},{1,129},{16,48},{17,145},{32,0},{33,161},{48,16},{49,177},{... | collective-permute-start | bytes 589832 | tf_op jit(solution)/shard_map/ppermute | solution.py:29
  12.2 0.2 shard_map.77
  12.5 0.3 collective-permute-start.1
  12.8 0.2 shard_map.78
  13.0 0.8 shard_map.79
  13.9 11.3 %collective-permute-start.2 = (bf16[48,2048]{1,0:T(8,128)(2,1)S(1)}, bf16[48,2048]{1,0:T(8,128)(2,1)S(1)}, u32[]{:S(2)}, u32[]{:S(2)}) collective-permute-start(bf16[48,2048]{1,0:T(8,128)(2,1)S(1)} %shard_map.78), channel_id=1, source_target_pairs={{0,48},{1,193},{16,0},{17,209},{32,16},{33,225},{48,32},{49,241},{... | collective-permute-start | bytes 589832 | tf_op jit(solution)/shard_map/ppermute | solution.py:29
  25.2 0.0 collective-permute-done.5
  25.2 0.0 collective-permute-done.3
  25.2 0.4 add_convert_fusion
  25.6 0.8 collective-permute-start.6
  26.4 1.1 %collective-permute-start.8 = (bf16[48,2048]{1,0:T(8,128)(2,1)S(1)}, bf16[48,2048]{1,0:T(8,128)(2,1)S(1)}, u32[]{:S(2)}, u32[]{:S(2)}) collective-permute-start(bf16[48,2048]{1,0:T(8,128)(2,1)S(1)} %get-tuple-element.11), channel_id=1, source_target_pairs={{0,192},{1,49},{16,208},{17,1},{32,224},{33,17},{48,240},{49,33},{... | collective-permute-start | bytes 589832 | tf_op jit(solution)/shard_map/ppermute | solution.py:29
  27.5 0.0 collective-permute-done
  27.5 1.0 collective-permute-start.7
  28.4 0.2 shard_map.75
  28.7 0.0 copy-start.2
  28.7 0.0 copy-start.3
  28.7 0.0 copy-start.4
  28.7 0.0 collective-permute-done.1
  28.7 1.7 %collective-permute-done.2 = bf16[48,2048]{1,0:T(8,128)(2,1)S(1)} collective-permute-done((bf16[48,2048]{1,0:T(8,128)(2,1)S(1)}, bf16[48,2048]{1,0:T(8,128)(2,1)S(1)}, u32[]{:S(2)}, u32[]{:S(2)}) %collective-permute-start.2) | collective-permute-done | bytes 196640 | tf_op jit(solution)/shard_map/ppermute | solution.py:29
  30.4 2.5 %collective-permute-done.6 = bf16[48,2048]{1,0:T(8,128)(2,1)S(1)} collective-permute-done((bf16[48,2048]{1,0:T(8,128)(2,1)S(1)}, bf16[48,2048]{1,0:T(8,128)(2,1)S(1)}, u32[]{:S(2)}, u32[]{:S(2)}) %collective-permute-start.6) | collective-permute-done | bytes 196640 | tf_op jit(solution)/shard_map/ppermute | solution.py:29
  32.9 2.0 %collective-permute-done.7 = bf16[48,2048]{1,0:T(8,128)(2,1)S(1)} collective-permute-done((bf16[48,2048]{1,0:T(8,128)(2,1)S(1)}, bf16[48,2048]{1,0:T(8,128)(2,1)S(1)}, u32[]{:S(2)}, u32[]{:S(2)}) %collective-permute-start.7) | collective-permute-done | bytes 196640 | tf_op jit(solution)/shard_map/ppermute | solution.py:29
  35.0 0.2 multiply_reduce_fusion
  35.2 15.4 %all_to_all.10 = f32[16,1,128]{2,1,0:T(1,128)S(1)} all-to-all(f32[16,1,128]{2,1,0:T(1,128)S(1)} %broadcast_in_dim.4), channel_id=1, replica_groups=mesh['dp_0'=4,'dp_1'=4,'shard_0'=8,'shard_1'=2] {'shard_0','shard_1'}, dimensions={0} | all-to-all | bytes 16384 | tf_op jit(solution)/shard_map/all_to_all | solution.py:106
  50.6 13.5 %all_to_all.11 = f32[16,1,128]{2,1,0:T(1,128)S(1)} all-to-all(f32[16,1,128]{2,1,0:T(1,128)S(1)} %broadcast_in_dim.5), channel_id=1, replica_groups=mesh['dp_0'=4,'dp_1'=4,'shard_0'=8,'shard_1'=2] {'dp_0','dp_1'}, dimensions={0} | all-to-all | bytes 16384 | tf_op jit(solution)/shard_map/all_to_all | solution.py:106
  64.1 0.6 reduce_sum.39
  65.4 1.2 %fusion.1 = (bf16[48,2048]{1,0:T(8,128)(2,1)S(1)}, f32[48,2048]{1,0:T(8,128)}, f32[48,2048]{1,0:T(8,128)}, f32[48,2048]{1,0:T(8,128)}) fusion(f32[48,2048]{1,0:T(8,128)S(1)} %copy-done.2, f32[48,2048]{1,0:T(8,128)S(1)} %get-tuple-element.9, f32[]{:T(128)S(6)} %min.4, f32[48,2048]{1,0:T(8,128)S(1)} %copy-done.3, f32[48,2048]{1,0:T(8,128)S(1)} %copy-done.4), kind=kLoop, calls=%fused_computation.11 | loop fusion | flops 1671168 | bytes 2949124 | tf_op jit(solution)/shard_map/convert_element_type | solution.py:165
  66.6 0.6 collective-permute-start.9
  67.2 2.7 %collective-permute-start.11 = (bf16[48,2048]{1,0:T(8,128)(2,1)S(1)}, bf16[48,2048]{1,0:T(8,128)(2,1)S(1)}, u32[]{:S(2)}, u32[]{:S(2)}) collective-permute-start(bf16[48,2048]{1,0:T(8,128)(2,1)S(1)} %get-tuple-element.4.refs_0_), channel_id=1, source_target_pairs={{0,192},{1,49},{16,208},{17,1},{32,224},{33,17},{48,240},{49,33},{... | collective-permute-start | bytes 589832 | tf_op jit(solution)/shard_map/ppermute | solution.py:29
  69.8 3.6 %collective-permute-done.9.refs_1_ = bf16[48,2048]{1,0:T(8,128)(2,1)S(1)} collective-permute-done((bf16[48,2048]{1,0:T(8,128)(2,1)S(1)}, bf16[48,2048]{1,0:T(8,128)(2,1)S(1)}, u32[]{:S(2)}, u32[]{:S(2)}) %collective-permute-start.9) | collective-permute-done | bytes 196640 | tf_op jit(solution)/shard_map/ppermute | solution.py:29
  73.5 3.5 %collective-permute-done.10.refs_2_ = bf16[48,2048]{1,0:T(8,128)(2,1)S(1)} collective-permute-done((bf16[48,2048]{1,0:T(8,128)(2,1)S(1)}, bf16[48,2048]{1,0:T(8,128)(2,1)S(1)}, u32[]{:S(2)}, u32[]{:S(2)}) %collective-permute-start.10) | collective-permute-done | bytes 196640 | tf_op jit(solution)/shard_map/ppermute | solution.py:29
  77.1 1.5 %collective-permute-start.14 = (bf16[144,2048]{1,0:T(8,128)(2,1)S(1)}, bf16[144,2048]{1,0:T(8,128)(2,1)S(1)}, u32[]{:S(2)}, u32[]{:S(2)}) collective-permute-start(bf16[144,2048]{1,0:T(8,128)(2,1)S(1)} %constant_dynamic-update-slice_fusion), channel_id=1, source_target_pairs={{0,48},{1,193},{16,0},{17,209},{32,16},{33,225},{48,32},{49,241},{... | collective-permute-start | bytes 1769480 | tf_op jit(solution)/shard_map/ppermute | solution.py:29
  78.6 0.6 collective-permute-start.13
  79.2 2.0 %collective-permute-start.12 = (bf16[144,2048]{1,0:T(8,128)(2,1)S(1)}, bf16[144,2048]{1,0:T(8,128)(2,1)S(1)}, u32[]{:S(2)}, u32[]{:S(2)}) collective-permute-start(bf16[144,2048]{1,0:T(8,128)(2,1)S(1)} %constant_dynamic-update-slice_fusion), channel_id=1, source_target_pairs={{0,16},{1,65},{16,32},{17,81},{32,48},{33,97},{48,0},{49,113},{64,... | collective-permute-start | bytes 1769480 | tf_op jit(solution)/shard_map/ppermute | solution.py:29
  81.3 2.9 %collective-permute-start.16 = (bf16[48,2048]{1,0:T(8,128)(2,1)S(1)}, bf16[48,2048]{1,0:T(8,128)(2,1)S(1)}, u32[]{:S(2)}, u32[]{:S(2)}) collective-permute-start(bf16[48,2048]{1,0:T(8,128)(2,1)S(1)} %get-tuple-element.4.refs_0_), channel_id=1, source_target_pairs={{0,32},{1,129},{16,48},{17,145},{32,0},{33,161},{48,16},{49,177},{... | collective-permute-start | bytes 589832 | tf_op jit(solution)/shard_map/ppermute | solution.py:29
  84.2 11.3 %collective-permute-done.17.refs_6_ = bf16[48,2048]{1,0:T(8,128)(2,1)S(1)} collective-permute-done((bf16[48,2048]{1,0:T(8,128)(2,1)S(1)}, bf16[48,2048]{1,0:T(8,128)(2,1)S(1)}, u32[]{:S(2)}, u32[]{:S(2)}) %collective-permute-start.17) | collective-permute-done | bytes 196640 | tf_op jit(solution)/shard_map/ppermute | solution.py:29
  95.5 0.6 collective-permute-start.15
  96.1 1.5 %collective-permute-done.16.refs_5_ = bf16[48,2048]{1,0:T(8,128)(2,1)S(1)} collective-permute-done((bf16[48,2048]{1,0:T(8,128)(2,1)S(1)}, bf16[48,2048]{1,0:T(8,128)(2,1)S(1)}, u32[]{:S(2)}, u32[]{:S(2)}) %collective-permute-start.16) | collective-permute-done | bytes 196640 | tf_op jit(solution)/shard_map/ppermute | solution.py:29
  97.6 3.5 %collective-permute-done.15.refs_4_ = bf16[48,2048]{1,0:T(8,128)(2,1)S(1)} collective-permute-done((bf16[48,2048]{1,0:T(8,128)(2,1)S(1)}, bf16[48,2048]{1,0:T(8,128)(2,1)S(1)}, u32[]{:S(2)}, u32[]{:S(2)}) %collective-permute-start.15) | collective-permute-done | bytes 196640 | tf_op jit(solution)/shard_map/ppermute | solution.py:29
  101.1 1.1 %shard_map.83.refs_3_ = bf16[768,2048]{1,0:T(8,128)(2,1)} custom-call(bf16[48,2048]{1,0:T(8,128)(2,1)S(1)} %get-tuple-element.4.refs_0_, bf16[48,2048]{1,0:T(8,128)(2,1)S(1)} %collective-permute-done.9.refs_1_, bf16[48,2048]{1,0:T(8,128)(2,1)S(1)} %collective-permute-done.10.refs_2_, bf16[48,2048]{1,0:T(8,128)(2,1)S(1)} %collective-permute-done.11.refs_3_, ...), custom_call_target="tpu_custom_call" | custom-call | flops 2000000 | bytes 2752512 | tf_op jit(solution)/shard_map/pallas_call | solution.py:89
  102.3 1.3 %shard_map.84 = bf16[768,2048]{1,0:T(8,128)(2,1)} custom-call(bf16[144,2048]{1,0:T(8,128)(2,1)S(1)} %collective-permute-done.12.refs_0_, bf16[144,2048]{1,0:T(8,128)(2,1)S(1)} %collective-permute-done.13.refs_1_, bf16[144,2048]{1,0:T(8,128)(2,1)S(1)} %collective-permute-done.14.refs_2_, ...), custom_call_target="tpu_custom_call", output_to_operand_aliasing={{}: (3, {})} | custom-call | flops 2000000 | bytes 3538944 | tf_op jit(solution)/shard_map/pallas_call | solution.py:89
  (22 shorter events, 0.2 us)
Async XLA Ops:
  0.6 1.9 %copy-start = (bf16[1,768,2048]{2,1,0:T(8,128)(2,1)S(1)}, bf16[1,768,2048]{2,1,0:T(8,128)(2,1)}, u32[]{:S(2)}) copy-start(bf16[1,768,2048]{2,1,0:T(8,128)(2,1)} %source.15) | copy-start | bytes 9437188
  2.5 2.4 %copy-start.1 = (bf16[1,768,2048]{2,1,0:T(8,128)(2,1)S(1)}, bf16[1,768,2048]{2,1,0:T(8,128)(2,1)}, u32[]{:S(2)}) copy-start(bf16[1,768,2048]{2,1,0:T(8,128)(2,1)} %source.15) | copy-start | bytes 9437188
  3.3 10.6 %collective-permute-start.4 = (bf16[144,2048]{1,0:T(8,128)(2,1)S(1)}, bf16[144,2048]{1,0:T(8,128)(2,1)S(1)}, u32[]{:S(2)}, u32[]{:S(2)}) collective-permute-start(bf16[144,2048]{1,0:T(8,128)(2,1)S(1)} %shard_map.81), channel_id=1, source_target_pairs={{0,16},{1,65},{16,32},{17,81},{32,48},{33,97},{48,0},{49,113},{64,... | collective-permute-start | bytes 1769480 | tf_op jit(solution)/shard_map/ppermute | solution.py:29
  5.7 19.5 %collective-permute-start.5 = (bf16[144,2048]{1,0:T(8,128)(2,1)S(1)}, bf16[144,2048]{1,0:T(8,128)(2,1)S(1)}, u32[]{:S(2)}, u32[]{:S(2)}) collective-permute-start(bf16[144,2048]{1,0:T(8,128)(2,1)S(1)} %shard_map.82), channel_id=1, source_target_pairs={{0,48},{1,193},{16,0},{17,209},{32,16},{33,225},{48,32},{49,241},{... | collective-permute-start | bytes 1769480 | tf_op jit(solution)/shard_map/ppermute | solution.py:29
  8.3 16.9 %collective-permute-start.3 = (bf16[144,2048]{1,0:T(8,128)(2,1)S(1)}, bf16[144,2048]{1,0:T(8,128)(2,1)S(1)}, u32[]{:S(2)}, u32[]{:S(2)}) collective-permute-start(bf16[144,2048]{1,0:T(8,128)(2,1)S(1)} %shard_map.80), channel_id=1, source_target_pairs={{0,32},{1,129},{16,48},{17,145},{32,0},{33,161},{48,16},{49,177},{... | collective-permute-start | bytes 1769480 | tf_op jit(solution)/shard_map/ppermute | solution.py:29
  9.7 17.7 %collective-permute-start = (bf16[48,2048]{1,0:T(8,128)(2,1)S(1)}, bf16[48,2048]{1,0:T(8,128)(2,1)S(1)}, u32[]{:S(2)}, u32[]{:S(2)}) collective-permute-start(bf16[48,2048]{1,0:T(8,128)(2,1)S(1)} %shard_map.76), channel_id=1, source_target_pairs={{0,32},{1,129},{16,48},{17,145},{32,0},{33,161},{48,16},{49,177},{... | collective-permute-start | bytes 589832 | tf_op jit(solution)/shard_map/ppermute | solution.py:29
  12.5 16.3 %collective-permute-start.1 = (bf16[48,2048]{1,0:T(8,128)(2,1)S(1)}, bf16[48,2048]{1,0:T(8,128)(2,1)S(1)}, u32[]{:S(2)}, u32[]{:S(2)}) collective-permute-start(bf16[48,2048]{1,0:T(8,128)(2,1)S(1)} %shard_map.77), channel_id=1, source_target_pairs={{0,16},{1,65},{16,32},{17,81},{32,48},{33,97},{48,0},{49,113},{64,... | collective-permute-start | bytes 589832 | tf_op jit(solution)/shard_map/ppermute | solution.py:29
  13.9 16.6 %collective-permute-start.2 = (bf16[48,2048]{1,0:T(8,128)(2,1)S(1)}, bf16[48,2048]{1,0:T(8,128)(2,1)S(1)}, u32[]{:S(2)}, u32[]{:S(2)}) collective-permute-start(bf16[48,2048]{1,0:T(8,128)(2,1)S(1)} %shard_map.78), channel_id=1, source_target_pairs={{0,48},{1,193},{16,0},{17,209},{32,16},{33,225},{48,32},{49,241},{... | collective-permute-start | bytes 589832 | tf_op jit(solution)/shard_map/ppermute | solution.py:29
  25.6 7.3 %collective-permute-start.6 = (bf16[48,2048]{1,0:T(8,128)(2,1)S(1)}, bf16[48,2048]{1,0:T(8,128)(2,1)S(1)}, u32[]{:S(2)}, u32[]{:S(2)}) collective-permute-start(bf16[48,2048]{1,0:T(8,128)(2,1)S(1)} %get-tuple-element.10), channel_id=1, source_target_pairs={{0,128},{1,33},{16,144},{17,49},{32,160},{33,1},{48,176},{49,17},{... | collective-permute-start | bytes 589832 | tf_op jit(solution)/shard_map/ppermute | solution.py:29
  26.4 6.5 %collective-permute-start.8 = (bf16[48,2048]{1,0:T(8,128)(2,1)S(1)}, bf16[48,2048]{1,0:T(8,128)(2,1)S(1)}, u32[]{:S(2)}, u32[]{:S(2)}) collective-permute-start(bf16[48,2048]{1,0:T(8,128)(2,1)S(1)} %get-tuple-element.11), channel_id=1, source_target_pairs={{0,192},{1,49},{16,208},{17,1},{32,224},{33,17},{48,240},{49,33},{... | collective-permute-start | bytes 589832 | tf_op jit(solution)/shard_map/ppermute | solution.py:29
  27.5 7.5 %collective-permute-start.7 = (bf16[48,2048]{1,0:T(8,128)(2,1)S(1)}, bf16[48,2048]{1,0:T(8,128)(2,1)S(1)}, u32[]{:S(2)}, u32[]{:S(2)}) collective-permute-start(bf16[48,2048]{1,0:T(8,128)(2,1)S(1)} %get-tuple-element.12), channel_id=1, source_target_pairs={{0,64},{1,17},{16,80},{17,33},{32,96},{33,49},{48,112},{49,1},{64,... | collective-permute-start | bytes 589832 | tf_op jit(solution)/shard_map/ppermute | solution.py:29
  28.7 36.7 %copy-start.2 = (f32[48,2048]{1,0:T(8,128)S(1)}, f32[48,2048]{1,0:T(8,128)}, u32[]{:S(2)}) copy-start(f32[48,2048]{1,0:T(8,128)} %param.5) | copy-start | bytes 1179652
  28.7 36.7 %copy-start.3 = (f32[48,2048]{1,0:T(8,128)S(1)}, f32[48,2048]{1,0:T(8,128)}, u32[]{:S(2)}) copy-start(f32[48,2048]{1,0:T(8,128)} %param.6) | copy-start | bytes 1179652
  28.7 36.7 %copy-start.4 = (f32[48,2048]{1,0:T(8,128)S(1)}, f32[48,2048]{1,0:T(8,128)}, u32[]{:S(2)}) copy-start(f32[48,2048]{1,0:T(8,128)} %param.7) | copy-start | bytes 1179652
  66.6 6.9 %collective-permute-start.9 = (bf16[48,2048]{1,0:T(8,128)(2,1)S(1)}, bf16[48,2048]{1,0:T(8,128)(2,1)S(1)}, u32[]{:S(2)}, u32[]{:S(2)}) collective-permute-start(bf16[48,2048]{1,0:T(8,128)(2,1)S(1)} %get-tuple-element.4.refs_0_), channel_id=1, source_target_pairs={{0,64},{1,17},{16,80},{17,33},{32,96},{33,49},{48,112},{49,1},{64,... | collective-permute-start | bytes 589832 | tf_op jit(solution)/shard_map/ppermute | solution.py:29
  67.2 9.9 %collective-permute-start.11 = (bf16[48,2048]{1,0:T(8,128)(2,1)S(1)}, bf16[48,2048]{1,0:T(8,128)(2,1)S(1)}, u32[]{:S(2)}, u32[]{:S(2)}) collective-permute-start(bf16[48,2048]{1,0:T(8,128)(2,1)S(1)} %get-tuple-element.4.refs_0_), channel_id=1, source_target_pairs={{0,192},{1,49},{16,208},{17,1},{32,224},{33,17},{48,240},{49,33},{... | collective-permute-start | bytes 589832 | tf_op jit(solution)/shard_map/ppermute | solution.py:29
  69.8 7.2 %collective-permute-start.10 = (bf16[48,2048]{1,0:T(8,128)(2,1)S(1)}, bf16[48,2048]{1,0:T(8,128)(2,1)S(1)}, u32[]{:S(2)}, u32[]{:S(2)}) collective-permute-start(bf16[48,2048]{1,0:T(8,128)(2,1)S(1)} %get-tuple-element.4.refs_0_), channel_id=1, source_target_pairs={{0,128},{1,33},{16,144},{17,49},{32,160},{33,1},{48,176},{49,17},{... | collective-permute-start | bytes 589832 | tf_op jit(solution)/shard_map/ppermute | solution.py:29
  77.1 25.2 %collective-permute-start.14 = (bf16[144,2048]{1,0:T(8,128)(2,1)S(1)}, bf16[144,2048]{1,0:T(8,128)(2,1)S(1)}, u32[]{:S(2)}, u32[]{:S(2)}) collective-permute-start(bf16[144,2048]{1,0:T(8,128)(2,1)S(1)} %constant_dynamic-update-slice_fusion), channel_id=1, source_target_pairs={{0,48},{1,193},{16,0},{17,209},{32,16},{33,225},{48,32},{49,241},{... | collective-permute-start | bytes 1769480 | tf_op jit(solution)/shard_map/ppermute | solution.py:29
  78.6 23.7 %collective-permute-start.13 = (bf16[144,2048]{1,0:T(8,128)(2,1)S(1)}, bf16[144,2048]{1,0:T(8,128)(2,1)S(1)}, u32[]{:S(2)}, u32[]{:S(2)}) collective-permute-start(bf16[144,2048]{1,0:T(8,128)(2,1)S(1)} %constant_dynamic-update-slice_fusion), channel_id=1, source_target_pairs={{0,32},{1,129},{16,48},{17,145},{32,0},{33,161},{48,16},{49,177},{... | collective-permute-start | bytes 1769480 | tf_op jit(solution)/shard_map/ppermute | solution.py:29
  79.2 23.1 %collective-permute-start.12 = (bf16[144,2048]{1,0:T(8,128)(2,1)S(1)}, bf16[144,2048]{1,0:T(8,128)(2,1)S(1)}, u32[]{:S(2)}, u32[]{:S(2)}) collective-permute-start(bf16[144,2048]{1,0:T(8,128)(2,1)S(1)} %constant_dynamic-update-slice_fusion), channel_id=1, source_target_pairs={{0,16},{1,65},{16,32},{17,81},{32,48},{33,97},{48,0},{49,113},{64,... | collective-permute-start | bytes 1769480 | tf_op jit(solution)/shard_map/ppermute | solution.py:29
  81.2 14.2 %collective-permute-start.17 = (bf16[48,2048]{1,0:T(8,128)(2,1)S(1)}, bf16[48,2048]{1,0:T(8,128)(2,1)S(1)}, u32[]{:S(2)}, u32[]{:S(2)}) collective-permute-start(bf16[48,2048]{1,0:T(8,128)(2,1)S(1)} %get-tuple-element.4.refs_0_), channel_id=1, source_target_pairs={{0,48},{1,193},{16,0},{17,209},{32,16},{33,225},{48,32},{49,241},{... | collective-permute-start | bytes 589832 | tf_op jit(solution)/shard_map/ppermute | solution.py:29
  81.3 16.4 %collective-permute-start.16 = (bf16[48,2048]{1,0:T(8,128)(2,1)S(1)}, bf16[48,2048]{1,0:T(8,128)(2,1)S(1)}, u32[]{:S(2)}, u32[]{:S(2)}) collective-permute-start(bf16[48,2048]{1,0:T(8,128)(2,1)S(1)} %get-tuple-element.4.refs_0_), channel_id=1, source_target_pairs={{0,32},{1,129},{16,48},{17,145},{32,0},{33,161},{48,16},{49,177},{... | collective-permute-start | bytes 589832 | tf_op jit(solution)/shard_map/ppermute | solution.py:29
  95.5 5.7 %collective-permute-start.15 = (bf16[48,2048]{1,0:T(8,128)(2,1)S(1)}, bf16[48,2048]{1,0:T(8,128)(2,1)S(1)}, u32[]{:S(2)}, u32[]{:S(2)}) collective-permute-start(bf16[48,2048]{1,0:T(8,128)(2,1)S(1)} %get-tuple-element.4.refs_0_), channel_id=1, source_target_pairs={{0,16},{1,65},{16,32},{17,81},{32,48},{33,97},{48,0},{49,113},{64,... | collective-permute-start | bytes 589832 | tf_op jit(solution)/shard_map/ppermute | solution.py:29

commit v2 on v1

--- a/solution.py
+++ b/solution.py
@@ -36,7 +36,7 @@
     return lax.rem(y + off_y, SIDE) * SIDE + lax.rem(x + off_x, SIDE)
 
 
-def picked(gradients, first, seconds, rows):
+def picked(gradients, first, seconds, rows, limit=1 << 20):
     width = gradients.shape[-1]
 
     def kernel(source, target, sems):
@@ -58,7 +58,7 @@
         in_specs=[pl.BlockSpec(memory_space=pltpu.HBM)],
         out_specs=pl.BlockSpec(memory_space=pl.ANY),
         scratch_shapes=[pltpu.SemaphoreType.DMA((count,))],
-        compiler_params=pltpu.CompilerParams(vmem_limit_bytes=1 << 20),
+        compiler_params=pltpu.CompilerParams(vmem_limit_bytes=limit),
         cost_estimate=pl.CostEstimate(
             flops=2000000, bytes_accessed=4 * count * rows * width, transcendentals=0
         ),
@@ -118,12 +118,42 @@
     return (new_master, new_first, new_second)
 
 
+def factor_of(square_sums, entries):
+    limit = 0.5 * math.sqrt(entries)
+    square_sum = jnp.sum(square_sums, axis=(0, 2))[:, None]
+    return jnp.minimum(1.0, limit / jnp.sqrt(square_sum + 1e-06))
+
+
+def updated(square_sums, entries, summed, *state, parameters):
+    def kernel(squares, summed, master, first, second, *outs):
+        factor = factor_of(squares[...], entries)
+        new = adam_update(summed[...], factor, master[...], first[...], second[...])
+        for out, value in zip(outs, new):
+            out[...] = value.astype(out.dtype)
+
+    vmem = pl.BlockSpec(memory_space=pltpu.VMEM)
+    dtypes = (jnp.bfloat16,) if parameters else (jnp.float32,) * 3
+    return pl.pallas_call(
+        kernel,
+        out_shape=[jax.ShapeDtypeStruct(summed.shape, dtype) for dtype in dtypes],
+        in_specs=[vmem] * 5,
+        out_specs=[vmem] * len(dtypes),
+        compiler_params=pltpu.CompilerParams(vmem_limit_bytes=8 << 20),
+        cost_estimate=pl.CostEstimate(
+            flops=2000000, bytes_accessed=18 * summed.size, transcendentals=2 * summed.size
+        ),
+        name="owned_parameters" if parameters else "new_state",
+    )(square_sums, summed, *state)
+
+
 def reduced(gradients, rows):
     f32 = jnp.float32
     onward = range(1, SIDE)
     passing = {}
     for d in (2, 1, 3):
-        passing[d] = moved(picked(gradients, d, onward, rows), 0, d).astype(f32)
+        limit = 55000000 if d == 2 else 1 << 20
+        block = picked(gradients, d, onward, rows, limit)
+        passing[d] = moved(block, 0, d).astype(f32)
     staying = {}
     for d in (2, 1, 3):
         staying[d] = moved(picked(gradients, d, (0,), rows), 0, d).astype(f32)
@@ -137,17 +167,28 @@
 
 
 def gathered(owned, rows):
-    nearby = {e: moved(owned, 1, e) for e in (2, 1, 3)}
-    along = {d: moved(owned, 0, d) for d in (2, 1, 3)}
-    held = jnp.concatenate([nearby[e] for e in (1, 2, 3)])
-    rest = {d: moved(held, 0, d) for d in (2, 1, 3)}
-    early = [owned] + [nearby[e] for e in (1, 2, 3)] + [along[d] for d in (1, 2, 3)]
-    places = [[(0, 0)]] + [[(0, -e)] for e in (1, 2, 3)] + [[(-d, 0)] for d in (1, 2, 3)]
-    places = [[(f % SIDE, s % SIDE) for f, s in p] for p in places]
-    out = placed(early, places, rows, None)
-    late = [rest[d] for d in (1, 2, 3)]
-    places = [[(-d % SIDE, -e % SIDE) for e in (1, 2, 3)] for d in (1, 2, 3)]
-    return placed(late, places, rows, out)
+    near = {e: moved(owned, 1, e) for e in (2, 1, 3)}
+    halves = ((0, 1), (2, 3))
+    blocks = {0: owned, **near}
+    held = [jnp.concatenate([blocks[e] for e in half]) for half in halves]
+    fore, back = [None] * 2, [None] * 2
+    for at in range(2):
+        fore[at] = moved(held[at], 0, 1)
+        back[1 - at] = moved(held[1 - at], 0, 3)
+    far = [moved(fore[0], 0, 1), moved(back[1], 0, 3)]
+
+    def places(first, half):
+        return [(first % SIDE, -e % SIDE) for e in halves[half]]
+
+    out = None
+    for pieces in (
+        [(held[0], 0, 0), (held[1], 0, 1), (fore[0], -1, 0), (back[1], 1, 1)],
+        [(fore[1], -1, 1), (back[0], 1, 0)],
+        [(far[0], -2, 0), (far[1], 2, 1)],
+    ):
+        at = [places(first, half) for _, first, half in pieces]
+        out = placed([piece for piece, _, _ in pieces], at, rows, out)
+    return out
 
 
 def step(gradients, master_weights, first_moment, second_moment):
@@ -156,14 +197,12 @@
     summed = reduced(gradients, rows)
     partial = jnp.sum(jnp.sum(summed * summed, axis=0).reshape(16, width // 16), axis=0)
     partial = jnp.sum(of_everyone(partial[None], SHARD), axis=0)
-    square_sum = jnp.sum(of_everyone(partial, DP), axis=(0, 2))[:, None]
-    limit = 0.5 * math.sqrt(entries)
-    factor = jnp.minimum(1.0, limit / jnp.sqrt(square_sum + 1e-06))
-    new_master, new_first, new_second = adam_update(
-        summed, factor, master_weights, first_moment, second_moment
-    )
-    parameters = gathered(new_master.astype(jnp.bfloat16), rows)
-    return (parameters, new_master, new_first, new_second)
+    squares = of_everyone(partial, DP)
+    state = (master_weights, first_moment, second_moment)
+    inputs = (squares, entries, summed, *state)
+    (owned,) = updated(*inputs, parameters=True)
+    parameters = gathered(owned, rows)
+    return (parameters, *updated(*inputs, parameters=False))
 
 
 def solution(mesh):

time: 105 us -> 90.7 us (0.86)
  the two profiles are of different devices: /device:TPU:2 before, /device:TPU:8 now
where the time goes in v2:
time: 90.7 us; the launch traced here: 90.6 us
  blocking collectives  30 us (33%)
  starting transfers between devices  25.7 us (28%)
  waiting for transfers between devices  23.3 us (26%)
  Pallas kernels  9.78 us (11%)
  between operations  1.01 us (1%)
    all_to_all x2, blocking collectives, of_everyone(): return lax.all_to_all(sent, axes, 0, 0, tiled=True)  30 us
    ppermute x18, starting transfers between devices, moved(): return lax.ppermute(array, PAIRED, pairs)  25.7 us
    ppermute x18, waiting for transfers between devices, moved(): return lax.ppermute(array, PAIRED, pairs)  23.3 us
    pallas_call x8, Pallas kernels, picked(): pl.pallas_call(kernel, out_shape=jax.ShapeDtypeStruct((count * rows, widt...  4.66 us
    pallas_call x3, Pallas kernels, placed(): pl.pallas_call(kernel, out_shape=jax.ShapeDtypeStruct((SIDE * SIDE * rows...  3 us
    pallas_call x2, Pallas kernels, updated(): pl.pallas_call(kernel, out_shape=[jax.ShapeDtypeStruct(summed.shape, dtyp...  2.11 us
  transfers between devices with their start and end apart: 18, of which 12 were waited for; matrix products, arithmetic and copies ran while one was open for 1% of the time, Pallas kernels for 8%

profile of v2, /device:TPU:8, one launch (start us, length us, event | category | flops | bytes accessed | tf_op | source)
XLA Modules:
  0.0 90.6 jit_solution(16283522070432947490)
XLA Ops:
  0.6 1.3 %shard_map.80 = bf16[144,2048]{1,0:T(8,128)(2,1)S(1)} custom-call(bf16[1,768,2048]{2,1,0:T(8,128)(2,1)} %source.15), custom_call_target="tpu_custom_call" | custom-call | flops 2000000 | bytes 1179648 | tf_op jit(solution)/shard_map/pallas_call | solution.py:55
  2.0 3.1 %collective-permute-start.3 = (bf16[144,2048]{1,0:T(8,128)(2,1)S(1)}, bf16[144,2048]{1,0:T(8,128)(2,1)S(1)}, u32[]{:S(2)}, u32[]{:S(2)}) collective-permute-start(bf16[144,2048]{1,0:T(8,128)(2,1)S(1)} %shard_map.80), channel_id=1, source_target_pairs={{0,32},{1,129},{16,48},{17,145},{32,0},{33,161},{48,16},{49,177},{... | collective-permute-start | bytes 1769480 | tf_op jit(solution)/shard_map/ppermute | solution.py:29
  5.1 0.8 shard_map.81
  5.9 0.7 collective-permute-start.4
  6.5 0.8 shard_map.82
  7.3 2.7 %collective-permute-start.5 = (bf16[144,2048]{1,0:T(8,128)(2,1)S(1)}, bf16[144,2048]{1,0:T(8,128)(2,1)S(1)}, u32[]{:S(2)}, u32[]{:S(2)}) collective-permute-start(bf16[144,2048]{1,0:T(8,128)(2,1)S(1)} %shard_map.82), channel_id=1, source_target_pairs={{0,48},{1,193},{16,0},{17,209},{32,16},{33,225},{48,32},{49,241},{... | collective-permute-start | bytes 1769480 | tf_op jit(solution)/shard_map/ppermute | solution.py:29
  10.0 0.2 shard_map.76
  10.3 0.1 collective-permute-start
  10.4 0.3 shard_map.77
  10.7 0.9 %collective-permute-start.1 = (bf16[48,2048]{1,0:T(8,128)(2,1)S(1)}, bf16[48,2048]{1,0:T(8,128)(2,1)S(1)}, u32[]{:S(2)}, u32[]{:S(2)}) collective-permute-start(bf16[48,2048]{1,0:T(8,128)(2,1)S(1)} %shard_map.77), channel_id=1, source_target_pairs={{0,16},{1,65},{16,32},{17,81},{32,48},{33,97},{48,0},{49,113},{64,... | collective-permute-start | bytes 589832 | tf_op jit(solution)/shard_map/ppermute | solution.py:29
  11.6 0.8 shard_map.79
  12.4 0.3 shard_map.78
  12.7 0.9 collective-permute-done.3
  13.5 2.8 %collective-permute-start.2 = (bf16[48,2048]{1,0:T(8,128)(2,1)S(1)}, bf16[48,2048]{1,0:T(8,128)(2,1)S(1)}, u32[]{:S(2)}, u32[]{:S(2)}) collective-permute-start(bf16[48,2048]{1,0:T(8,128)(2,1)S(1)} %shard_map.78), channel_id=1, source_target_pairs={{0,48},{1,193},{16,0},{17,209},{32,16},{33,225},{48,32},{49,241},{... | collective-permute-start | bytes 589832 | tf_op jit(solution)/shard_map/ppermute | solution.py:29
  16.3 3.5 %collective-permute-done.4 = bf16[144,2048]{1,0:T(8,128)(2,1)S(1)} collective-permute-done((bf16[144,2048]{1,0:T(8,128)(2,1)S(1)}, bf16[144,2048]{1,0:T(8,128)(2,1)S(1)}, u32[]{:S(2)}, u32[]{:S(2)}) %collective-permute-start.4) | collective-permute-done | bytes 589856 | tf_op jit(solution)/shard_map/ppermute | solution.py:29
  19.8 0.1 collective-permute-done.5
  19.8 0.4 add_convert_fusion
  20.3 2.4 %collective-permute-start.6 = (bf16[48,2048]{1,0:T(8,128)(2,1)S(1)}, bf16[48,2048]{1,0:T(8,128)(2,1)S(1)}, u32[]{:S(2)}, u32[]{:S(2)}) collective-permute-start(bf16[48,2048]{1,0:T(8,128)(2,1)S(1)} %get-tuple-element.12), channel_id=1, source_target_pairs={{0,128},{1,33},{16,144},{17,49},{32,160},{33,1},{48,176},{49,17},{... | collective-permute-start | bytes 589832 | tf_op jit(solution)/shard_map/ppermute | solution.py:29
  22.7 1.2 %collective-permute-start.7 = (bf16[48,2048]{1,0:T(8,128)(2,1)S(1)}, bf16[48,2048]{1,0:T(8,128)(2,1)S(1)}, u32[]{:S(2)}, u32[]{:S(2)}) collective-permute-start(bf16[48,2048]{1,0:T(8,128)(2,1)S(1)} %get-tuple-element.14), channel_id=1, source_target_pairs={{0,64},{1,17},{16,80},{17,33},{32,96},{33,49},{48,112},{49,1},{64,... | collective-permute-start | bytes 589832 | tf_op jit(solution)/shard_map/ppermute | solution.py:29
  23.9 0.8 collective-permute-start.8
  24.7 0.2 shard_map.75
  24.9 0.0 copy-start.1
  25.0 2.6 %collective-permute-done.6 = bf16[48,2048]{1,0:T(8,128)(2,1)S(1)} collective-permute-done((bf16[48,2048]{1,0:T(8,128)(2,1)S(1)}, bf16[48,2048]{1,0:T(8,128)(2,1)S(1)}, u32[]{:S(2)}, u32[]{:S(2)}) %collective-permute-start.6) | collective-permute-done | bytes 196640 | tf_op jit(solution)/shard_map/ppermute | solution.py:29
  27.6 2.2 %collective-permute-done.7 = bf16[48,2048]{1,0:T(8,128)(2,1)S(1)} collective-permute-done((bf16[48,2048]{1,0:T(8,128)(2,1)S(1)}, bf16[48,2048]{1,0:T(8,128)(2,1)S(1)}, u32[]{:S(2)}, u32[]{:S(2)}) %collective-permute-start.7) | collective-permute-done | bytes 196640 | tf_op jit(solution)/shard_map/ppermute | solution.py:29
  29.8 0.2 multiply_reduce_fusion
  30.0 16.0 %all_to_all.10 = f32[16,1,128]{2,1,0:T(1,128)S(1)} all-to-all(f32[16,1,128]{2,1,0:T(1,128)S(1)} %broadcast_in_dim.4), channel_id=1, replica_groups=mesh['dp_0'=4,'dp_1'=4,'shard_0'=8,'shard_1'=2] {'shard_0','shard_1'}, dimensions={0} | all-to-all | bytes 16384 | tf_op jit(solution)/shard_map/all_to_all | solution.py:106
  46.1 14.0 %all_to_all.11.squares = f32[16,1,128]{2,1,0:T(1,128)S(1)} all-to-all(f32[16,1,128]{2,1,0:T(1,128)S(1)} %broadcast_in_dim.5), channel_id=1, replica_groups=mesh['dp_0'=4,'dp_1'=4,'shard_0'=8,'shard_1'=2] {'dp_0','dp_1'}, dimensions={0} | all-to-all | bytes 16384 | tf_op jit(solution)/shard_map/all_to_all | solution.py:106
  60.1 0.7 owned_parameters.1
  60.8 1.5 %collective-permute-start.12 = (bf16[48,2048]{1,0:T(8,128)(2,1)S(1)}, bf16[48,2048]{1,0:T(8,128)(2,1)S(1)}, u32[]{:S(2)}, u32[]{:S(2)}) collective-permute-start(bf16[48,2048]{1,0:T(8,128)(2,1)S(1)} %owned_parameters.1), channel_id=1, source_target_pairs={{0,128},{1,33},{16,144},{17,49},{32,160},{33,1},{48,176},{49,17},{... | collective-permute-start | bytes 589832 | tf_op jit(solution)/shard_map/ppermute | solution.py:29
  62.3 1.2 %collective-permute-start.13 = (bf16[48,2048]{1,0:T(8,128)(2,1)S(1)}, bf16[48,2048]{1,0:T(8,128)(2,1)S(1)}, u32[]{:S(2)}, u32[]{:S(2)}) collective-permute-start(bf16[48,2048]{1,0:T(8,128)(2,1)S(1)} %owned_parameters.1), channel_id=1, source_target_pairs={{0,192},{1,49},{16,208},{17,1},{32,224},{33,17},{48,240},{49,33},{... | collective-permute-start | bytes 589832 | tf_op jit(solution)/shard_map/ppermute | solution.py:29
  63.5 0.8 collective-permute-start.9
  64.3 3.8 %collective-permute-done.12 = bf16[48,2048]{1,0:T(8,128)(2,1)S(1)} collective-permute-done((bf16[48,2048]{1,0:T(8,128)(2,1)S(1)}, bf16[48,2048]{1,0:T(8,128)(2,1)S(1)}, u32[]{:S(2)}, u32[]{:S(2)}) %collective-permute-start.12) | collective-permute-done | bytes 196640 | tf_op jit(solution)/shard_map/ppermute | solution.py:29
  68.2 3.1 %collective-permute-done.13 = bf16[48,2048]{1,0:T(8,128)(2,1)S(1)} collective-permute-done((bf16[48,2048]{1,0:T(8,128)(2,1)S(1)}, bf16[48,2048]{1,0:T(8,128)(2,1)S(1)}, u32[]{:S(2)}, u32[]{:S(2)}) %collective-permute-start.13) | collective-permute-done | bytes 196640 | tf_op jit(solution)/shard_map/ppermute | solution.py:29
  71.3 0.1 collective-permute-start.14
  71.4 2.1 %collective-permute-start.10 = (bf16[96,2048]{1,0:T(8,128)(2,1)S(1)}, bf16[96,2048]{1,0:T(8,128)(2,1)S(1)}, u32[]{:S(2)}, u32[]{:S(2)}) collective-permute-start(bf16[96,2048]{1,0:T(8,128)(2,1)S(1)} %pad_maximum_fusion.refs_0_), channel_id=1, source_target_pairs={{0,16},{1,65},{16,32},{17,81},{32,48},{33,97},{48,0},{49,113},{64,... | collective-permute-start | bytes 1179656 | tf_op jit(solution)/shard_map/ppermute | solution.py:29
  73.5 0.3 collective-permute-start.16
  73.8 3.0 %collective-permute-start.17 = (bf16[96,2048]{1,0:T(8,128)(2,1)S(1)}, bf16[96,2048]{1,0:T(8,128)(2,1)S(1)}, u32[]{:S(2)}, u32[]{:S(2)}) collective-permute-start(bf16[96,2048]{1,0:T(8,128)(2,1)S(1)} %pad_maximum_fusion.refs_0_), channel_id=1, source_target_pairs={{0,48},{1,193},{16,0},{17,209},{32,16},{33,225},{48,32},{49,241},{... | collective-permute-start | bytes 1179656 | tf_op jit(solution)/shard_map/ppermute | solution.py:29
  76.8 2.4 %collective-permute-done.14.refs_3_ = bf16[96,2048]{1,0:T(8,128)(2,1)S(1)} collective-permute-done((bf16[96,2048]{1,0:T(8,128)(2,1)S(1)}, bf16[96,2048]{1,0:T(8,128)(2,1)S(1)}, u32[]{:S(2)}, u32[]{:S(2)}) %collective-permute-start.14) | collective-permute-done | bytes 393248 | tf_op jit(solution)/shard_map/ppermute | solution.py:29
  79.2 1.2 %collective-permute-start.15 = (bf16[96,2048]{1,0:T(8,128)(2,1)S(1)}, bf16[96,2048]{1,0:T(8,128)(2,1)S(1)}, u32[]{:S(2)}, u32[]{:S(2)}) collective-permute-start(bf16[96,2048]{1,0:T(8,128)(2,1)S(1)} %collective-permute-done.14.refs_3_), channel_id=1, source_target_pairs={{0,48},{1,193},{16,0},{17,209},{32,16},{33,225},{48,32},{49,241},{... | collective-permute-start | bytes 1179656 | tf_op jit(solution)/shard_map/ppermute | solution.py:29
  80.4 0.1 collective-permute-done.10.refs_2_
  80.5 0.8 collective-permute-start.11
  81.3 1.4 %new_state.1 = (f32[48,2048]{1,0:T(8,128)}, f32[48,2048]{1,0:T(8,128)}, f32[48,2048]{1,0:T(8,128)}) custom-call(f32[16,1,128]{2,1,0:T(1,128)S(1)} %all_to_all.11.squares, f32[48,2048]{1,0:T(8,128)S(1)} %get-tuple-element.11.summed, f32[48,2048]{1,0:T(8,128)S(1)} %copy-done.1, f32[48,2048]{1,0:T(8,128)S(1)} %copy-done.2, f32[48,2048]{1,0:T(8,128)S(1)} %copy-done.3), custom_call_target="tpu_custom_call" | custom-call | flops 2000000 | bytes 1769472 | tf_op jit(solution)/shard_map/new_state/pallas_call | solution.py:136
  82.7 1.2 %shard_map.83.refs_2_ = bf16[768,2048]{1,0:T(8,128)(2,1)} custom-call(bf16[96,2048]{1,0:T(8,128)(2,1)S(1)} %pad_maximum_fusion.refs_0_, bf16[96,2048]{1,0:T(8,128)(2,1)S(1)} %constant_dynamic-update-slice_fusion.refs_1_, bf16[96,2048]{1,0:T(8,128)(2,1)S(1)} %collective-permute-done.10.refs_2_, bf16[96,2048]{1,0:T(8,128)(2,1)S(1)} %collective-permute-done.14.refs_3_), custom_call_target="tpu_custom_call" | custom-call | flops 2000000 | bytes 3145728 | tf_op jit(solution)/shard_map/pallas_call | solution.py:89
  83.9 0.8 collective-permute-done.16.refs_0_
  84.7 0.9 shard_map.84.refs_2_
  85.6 1.9 %collective-permute-done.15.refs_1_ = bf16[96,2048]{1,0:T(8,128)(2,1)S(1)} collective-permute-done((bf16[96,2048]{1,0:T(8,128)(2,1)S(1)}, bf16[96,2048]{1,0:T(8,128)(2,1)S(1)}, u32[]{:S(2)}, u32[]{:S(2)}) %collective-permute-start.15) | collective-permute-done | bytes 393248 | tf_op jit(solution)/shard_map/ppermute | solution.py:29
  87.6 1.9 %collective-permute-done.11.refs_0_ = bf16[96,2048]{1,0:T(8,128)(2,1)S(1)} collective-permute-done((bf16[96,2048]{1,0:T(8,128)(2,1)S(1)}, bf16[96,2048]{1,0:T(8,128)(2,1)S(1)}, u32[]{:S(2)}, u32[]{:S(2)}) %collective-permute-start.11) | collective-permute-done | bytes 393248 | tf_op jit(solution)/shard_map/ppermute | solution.py:29
  89.5 0.9 shard_map.85
  (21 shorter events, 0.2 us)
Async XLA Ops:
  0.6 4.4 %copy-start = (bf16[1,768,2048]{2,1,0:T(8,128)(2,1)S(1)}, bf16[1,768,2048]{2,1,0:T(8,128)(2,1)}, u32[]{:S(2)}) copy-start(bf16[1,768,2048]{2,1,0:T(8,128)(2,1)} %source.15) | copy-start | bytes 9437188
  2.0 11.6 %collective-permute-start.3 = (bf16[144,2048]{1,0:T(8,128)(2,1)S(1)}, bf16[144,2048]{1,0:T(8,128)(2,1)S(1)}, u32[]{:S(2)}, u32[]{:S(2)}) collective-permute-start(bf16[144,2048]{1,0:T(8,128)(2,1)S(1)} %shard_map.80), channel_id=1, source_target_pairs={{0,32},{1,129},{16,48},{17,145},{32,0},{33,161},{48,16},{49,177},{... | collective-permute-start | bytes 1769480 | tf_op jit(solution)/shard_map/ppermute | solution.py:29
  5.9 13.9 %collective-permute-start.4 = (bf16[144,2048]{1,0:T(8,128)(2,1)S(1)}, bf16[144,2048]{1,0:T(8,128)(2,1)S(1)}, u32[]{:S(2)}, u32[]{:S(2)}) collective-permute-start(bf16[144,2048]{1,0:T(8,128)(2,1)S(1)} %shard_map.81), channel_id=1, source_target_pairs={{0,16},{1,65},{16,32},{17,81},{32,48},{33,97},{48,0},{49,113},{64,... | collective-permute-start | bytes 1769480 | tf_op jit(solution)/shard_map/ppermute | solution.py:29
  7.3 12.5 %collective-permute-start.5 = (bf16[144,2048]{1,0:T(8,128)(2,1)S(1)}, bf16[144,2048]{1,0:T(8,128)(2,1)S(1)}, u32[]{:S(2)}, u32[]{:S(2)}) collective-permute-start(bf16[144,2048]{1,0:T(8,128)(2,1)S(1)} %shard_map.82), channel_id=1, source_target_pairs={{0,48},{1,193},{16,0},{17,209},{32,16},{33,225},{48,32},{49,241},{... | collective-permute-start | bytes 1769480 | tf_op jit(solution)/shard_map/ppermute | solution.py:29
  10.3 13.6 %collective-permute-start = (bf16[48,2048]{1,0:T(8,128)(2,1)S(1)}, bf16[48,2048]{1,0:T(8,128)(2,1)S(1)}, u32[]{:S(2)}, u32[]{:S(2)}) collective-permute-start(bf16[48,2048]{1,0:T(8,128)(2,1)S(1)} %shard_map.76), channel_id=1, source_target_pairs={{0,32},{1,129},{16,48},{17,145},{32,0},{33,161},{48,16},{49,177},{... | collective-permute-start | bytes 589832 | tf_op jit(solution)/shard_map/ppermute | solution.py:29
  10.7 14.3 %collective-permute-start.1 = (bf16[48,2048]{1,0:T(8,128)(2,1)S(1)}, bf16[48,2048]{1,0:T(8,128)(2,1)S(1)}, u32[]{:S(2)}, u32[]{:S(2)}) collective-permute-start(bf16[48,2048]{1,0:T(8,128)(2,1)S(1)} %shard_map.77), channel_id=1, source_target_pairs={{0,16},{1,65},{16,32},{17,81},{32,48},{33,97},{48,0},{49,113},{64,... | collective-permute-start | bytes 589832 | tf_op jit(solution)/shard_map/ppermute | solution.py:29
  13.5 11.5 %collective-permute-start.2 = (bf16[48,2048]{1,0:T(8,128)(2,1)S(1)}, bf16[48,2048]{1,0:T(8,128)(2,1)S(1)}, u32[]{:S(2)}, u32[]{:S(2)}) collective-permute-start(bf16[48,2048]{1,0:T(8,128)(2,1)S(1)} %shard_map.78), channel_id=1, source_target_pairs={{0,48},{1,193},{16,0},{17,209},{32,16},{33,225},{48,32},{49,241},{... | collective-permute-start | bytes 589832 | tf_op jit(solution)/shard_map/ppermute | solution.py:29
  20.3 7.3 %collective-permute-start.6 = (bf16[48,2048]{1,0:T(8,128)(2,1)S(1)}, bf16[48,2048]{1,0:T(8,128)(2,1)S(1)}, u32[]{:S(2)}, u32[]{:S(2)}) collective-permute-start(bf16[48,2048]{1,0:T(8,128)(2,1)S(1)} %get-tuple-element.12), channel_id=1, source_target_pairs={{0,128},{1,33},{16,144},{17,49},{32,160},{33,1},{48,176},{49,17},{... | collective-permute-start | bytes 589832 | tf_op jit(solution)/shard_map/ppermute | solution.py:29
  22.7 7.1 %collective-permute-start.7 = (bf16[48,2048]{1,0:T(8,128)(2,1)S(1)}, bf16[48,2048]{1,0:T(8,128)(2,1)S(1)}, u32[]{:S(2)}, u32[]{:S(2)}) collective-permute-start(bf16[48,2048]{1,0:T(8,128)(2,1)S(1)} %get-tuple-element.14), channel_id=1, source_target_pairs={{0,64},{1,17},{16,80},{17,33},{32,96},{33,49},{48,112},{49,1},{64,... | collective-permute-start | bytes 589832 | tf_op jit(solution)/shard_map/ppermute | solution.py:29
  23.9 5.9 %collective-permute-start.8 = (bf16[48,2048]{1,0:T(8,128)(2,1)S(1)}, bf16[48,2048]{1,0:T(8,128)(2,1)S(1)}, u32[]{:S(2)}, u32[]{:S(2)}) collective-permute-start(bf16[48,2048]{1,0:T(8,128)(2,1)S(1)} %get-tuple-element.13), channel_id=1, source_target_pairs={{0,192},{1,49},{16,208},{17,1},{32,224},{33,17},{48,240},{49,33},{... | collective-permute-start | bytes 589832 | tf_op jit(solution)/shard_map/ppermute | solution.py:29
  24.9 35.1 %copy-start.1 = (f32[48,2048]{1,0:T(8,128)S(1)}, f32[48,2048]{1,0:T(8,128)}, u32[]{:S(2)}) copy-start(f32[48,2048]{1,0:T(8,128)} %master.3) | copy-start | bytes 1179652
  24.9 35.1 %copy-start.2 = (f32[48,2048]{1,0:T(8,128)S(1)}, f32[48,2048]{1,0:T(8,128)}, u32[]{:S(2)}) copy-start(f32[48,2048]{1,0:T(8,128)} %first.3) | copy-start | bytes 1179652
  25.0 35.1 %copy-start.3 = (f32[48,2048]{1,0:T(8,128)S(1)}, f32[48,2048]{1,0:T(8,128)}, u32[]{:S(2)}) copy-start(f32[48,2048]{1,0:T(8,128)} %second.3) | copy-start | bytes 1179652
  60.8 7.4 %collective-permute-start.12 = (bf16[48,2048]{1,0:T(8,128)(2,1)S(1)}, bf16[48,2048]{1,0:T(8,128)(2,1)S(1)}, u32[]{:S(2)}, u32[]{:S(2)}) collective-permute-start(bf16[48,2048]{1,0:T(8,128)(2,1)S(1)} %owned_parameters.1), channel_id=1, source_target_pairs={{0,128},{1,33},{16,144},{17,49},{32,160},{33,1},{48,176},{49,17},{... | collective-permute-start | bytes 589832 | tf_op jit(solution)/shard_map/ppermute | solution.py:29
  62.3 9.0 %collective-permute-start.13 = (bf16[48,2048]{1,0:T(8,128)(2,1)S(1)}, bf16[48,2048]{1,0:T(8,128)(2,1)S(1)}, u32[]{:S(2)}, u32[]{:S(2)}) collective-permute-start(bf16[48,2048]{1,0:T(8,128)(2,1)S(1)} %owned_parameters.1), channel_id=1, source_target_pairs={{0,192},{1,49},{16,208},{17,1},{32,224},{33,17},{48,240},{49,33},{... | collective-permute-start | bytes 589832 | tf_op jit(solution)/shard_map/ppermute | solution.py:29
  63.5 7.9 %collective-permute-start.9 = (bf16[48,2048]{1,0:T(8,128)(2,1)S(1)}, bf16[48,2048]{1,0:T(8,128)(2,1)S(1)}, u32[]{:S(2)}, u32[]{:S(2)}) collective-permute-start(bf16[48,2048]{1,0:T(8,128)(2,1)S(1)} %owned_parameters.1), channel_id=1, source_target_pairs={{0,64},{1,17},{16,80},{17,33},{32,96},{33,49},{48,112},{49,1},{64,... | collective-permute-start | bytes 589832 | tf_op jit(solution)/shard_map/ppermute | solution.py:29
  71.3 7.9 %collective-permute-start.14 = (bf16[96,2048]{1,0:T(8,128)(2,1)S(1)}, bf16[96,2048]{1,0:T(8,128)(2,1)S(1)}, u32[]{:S(2)}, u32[]{:S(2)}) collective-permute-start(bf16[96,2048]{1,0:T(8,128)(2,1)S(1)} %constant_dynamic-update-slice_fusion.refs_1_), channel_id=1, source_target_pairs={{0,48},{1,193},{16,0},{17,209},{32,16},{33,225},{48,32},{49,241},{... | collective-permute-start | bytes 1179656 | tf_op jit(solution)/shard_map/ppermute | solution.py:29
  71.4 9.1 %collective-permute-start.10 = (bf16[96,2048]{1,0:T(8,128)(2,1)S(1)}, bf16[96,2048]{1,0:T(8,128)(2,1)S(1)}, u32[]{:S(2)}, u32[]{:S(2)}) collective-permute-start(bf16[96,2048]{1,0:T(8,128)(2,1)S(1)} %pad_maximum_fusion.refs_0_), channel_id=1, source_target_pairs={{0,16},{1,65},{16,32},{17,81},{32,48},{33,97},{48,0},{49,113},{64,... | collective-permute-start | bytes 1179656 | tf_op jit(solution)/shard_map/ppermute | solution.py:29
  73.5 11.2 %collective-permute-start.16 = (bf16[96,2048]{1,0:T(8,128)(2,1)S(1)}, bf16[96,2048]{1,0:T(8,128)(2,1)S(1)}, u32[]{:S(2)}, u32[]{:S(2)}) collective-permute-start(bf16[96,2048]{1,0:T(8,128)(2,1)S(1)} %constant_dynamic-update-slice_fusion.refs_1_), channel_id=1, source_target_pairs={{0,16},{1,65},{16,32},{17,81},{32,48},{33,97},{48,0},{49,113},{64,... | collective-permute-start | bytes 1179656 | tf_op jit(solution)/shard_map/ppermute | solution.py:29
  73.8 10.9 %collective-permute-start.17 = (bf16[96,2048]{1,0:T(8,128)(2,1)S(1)}, bf16[96,2048]{1,0:T(8,128)(2,1)S(1)}, u32[]{:S(2)}, u32[]{:S(2)}) collective-permute-start(bf16[96,2048]{1,0:T(8,128)(2,1)S(1)} %pad_maximum_fusion.refs_0_), channel_id=1, source_target_pairs={{0,48},{1,193},{16,0},{17,209},{32,16},{33,225},{48,32},{49,241},{... | collective-permute-start | bytes 1179656 | tf_op jit(solution)/shard_map/ppermute | solution.py:29
  79.2 8.4 %collective-permute-start.15 = (bf16[96,2048]{1,0:T(8,128)(2,1)S(1)}, bf16[96,2048]{1,0:T(8,128)(2,1)S(1)}, u32[]{:S(2)}, u32[]{:S(2)}) collective-permute-start(bf16[96,2048]{1,0:T(8,128)(2,1)S(1)} %collective-permute-done.14.refs_3_), channel_id=1, source_target_pairs={{0,48},{1,193},{16,0},{17,209},{32,16},{33,225},{48,32},{49,241},{... | collective-permute-start | bytes 1179656 | tf_op jit(solution)/shard_map/ppermute | solution.py:29
  80.5 9.0 %collective-permute-start.11 = (bf16[96,2048]{1,0:T(8,128)(2,1)S(1)}, bf16[96,2048]{1,0:T(8,128)(2,1)S(1)}, u32[]{:S(2)}, u32[]{:S(2)}) collective-permute-start(bf16[96,2048]{1,0:T(8,128)(2,1)S(1)} %collective-permute-done.10.refs_2_), channel_id=1, source_target_pairs={{0,16},{1,65},{16,32},{17,81},{32,48},{33,97},{48,0},{49,113},{64,... | collective-permute-start | bytes 1179656 | tf_op jit(solution)/shard_map/ppermute | solution.py:29

commit v3 on v2

--- a/solution.py
+++ b/solution.py
@@ -13,6 +13,7 @@
 SHARD_DP = ("shard_0", "shard_1", "dp_0", "dp_1")
 PAIRED = ("dp_0", "dp_1", "shard_1")
 SIDE = 4
+PIECE = 1024
 
 
 first_bias = 1.0 - math.exp(100.0 * math.log(0.9))
@@ -24,7 +25,7 @@
     for y in range(SIDE):
         for x in range(SIDE):
             for core in range(2):
-                to_y, to_x = (y, (x + by) % SIDE) if axis == core else ((y + by) % SIDE, x)
+                to_y, to_x = (y, x ^ by) if axis == core else (y ^ by, x)
                 pairs.append(((y * SIDE + x) * 2 + core, (to_y * SIDE + to_x) * 2 + core))
     return lax.ppermute(array, PAIRED, pairs)
 
@@ -33,7 +34,7 @@
     y, x, core = (lax.axis_index(name) for name in ("dp_0", "dp_1", "shard_1"))
     off_x = jnp.where(core == 0, first, second)
     off_y = jnp.where(core == 0, second, first)
-    return lax.rem(y + off_y, SIDE) * SIDE + lax.rem(x + off_x, SIDE)
+    return (y ^ off_y) * SIDE + (x ^ off_x)
 
 
 def picked(gradients, first, seconds, rows, limit=1 << 20):
@@ -43,11 +44,14 @@
         copies = []
         for i, second in enumerate(seconds):
             at = pl.multiple_of(block_at(first, second) * rows, rows)
-            copy = pltpu.make_async_copy(
-                source.at[0, pl.ds(at, rows)], target.at[pl.ds(i * rows, rows)], sems.at[i]
-            )
-            copy.start()
-            copies.append(copy)
+            for left in range(0, width, PIECE):
+                copy = pltpu.make_async_copy(
+                    source.at[0, pl.ds(at, rows), pl.ds(left, PIECE)],
+                    target.at[pl.ds(i * rows, rows), pl.ds(left, PIECE)],
+                    sems.at[len(copies)],
+                )
+                copy.start()
+                copies.append(copy)
         for copy in copies:
             copy.wait()
 
@@ -57,7 +61,7 @@
         out_shape=jax.ShapeDtypeStruct((count * rows, width), gradients.dtype),
         in_specs=[pl.BlockSpec(memory_space=pltpu.HBM)],
         out_specs=pl.BlockSpec(memory_space=pl.ANY),
-        scratch_shapes=[pltpu.SemaphoreType.DMA((count,))],
+        scratch_shapes=[pltpu.SemaphoreType.DMA((count * (width // PIECE),))],
         compiler_params=pltpu.CompilerParams(vmem_limit_bytes=limit),
         cost_estimate=pl.CostEstimate(
             flops=2000000, bytes_accessed=4 * count * rows * width, transcendentals=0
@@ -175,16 +179,16 @@
     for at in range(2):
         fore[at] = moved(held[at], 0, 1)
         back[1 - at] = moved(held[1 - at], 0, 3)
-    far = [moved(fore[0], 0, 1), moved(back[1], 0, 3)]
+    far = [moved(fore[0], 0, 3), moved(back[1], 0, 1)]
 
     def places(first, half):
-        return [(first % SIDE, -e % SIDE) for e in halves[half]]
+        return [(first, e) for e in halves[half]]
 
     out = None
     for pieces in (
-        [(held[0], 0, 0), (held[1], 0, 1), (fore[0], -1, 0), (back[1], 1, 1)],
-        [(fore[1], -1, 1), (back[0], 1, 0)],
-        [(far[0], -2, 0), (far[1], 2, 1)],
+        [(held[0], 0, 0), (held[1], 0, 1), (fore[0], 1, 0), (back[1], 3, 1)],
+        [(fore[1], 1, 1), (back[0], 3, 0)],
+        [(far[0], 2, 0), (far[1], 2, 1)],
     ):
         at = [places(first, half) for _, first, half in pieces]
         out = placed([piece for piece, _, _ in pieces], at, rows, out)

time: 90.7 us -> 88.9 us (0.980)
  the two profiles are of different devices: /device:TPU:8 before, /device:TPU:2 now
where the time goes in v3:
time: 88.9 us; the launch traced here: 88.7 us
  blocking collectives  27.9 us (31%)
  waiting for transfers between devices  26.3 us (30%)
  starting transfers between devices  25.5 us (29%)
  Pallas kernels  7.31 us (8%)
    all_to_all x2, blocking collectives, of_everyone(): return lax.all_to_all(sent, axes, 0, 0, tiled=True)  27.9 us
    ppermute x18, waiting for transfers between devices, moved(): return lax.ppermute(array, PAIRED, pairs)  26.3 us
    ppermute x18, starting transfers between devices, moved(): return lax.ppermute(array, PAIRED, pairs)  25.5 us
    pallas_call x3, Pallas kernels, placed(): pl.pallas_call(kernel, out_shape=jax.ShapeDtypeStruct((SIDE * SIDE * rows...  3.03 us
    pallas_call x8, Pallas kernels, picked(): pl.pallas_call(kernel, out_shape=jax.ShapeDtypeStruct((count * rows, widt...  2.18 us
    pallas_call x2, Pallas kernels, updated(): pl.pallas_call(kernel, out_shape=[jax.ShapeDtypeStruct(summed.shape, dtyp...  2.11 us
  transfers between devices with their start and end apart: 18, of which 10 were waited for; matrix products, arithmetic and copies ran while one was open for 1% of the time, Pallas kernels for 5%

profile of v3, /device:TPU:2, one launch (start us, length us, event | category | flops | bytes accessed | tf_op | source)
XLA Modules:
  0.0 88.7 jit_solution(4048371802733079894)
XLA Ops:
  0.6 1.3 %shard_map.80 = bf16[144,2048]{1,0:T(8,128)(2,1)S(1)} custom-call(bf16[1,768,2048]{2,1,0:T(8,128)(2,1)} %source.15), custom_call_target="tpu_custom_call" | custom-call | flops 2000000 | bytes 1179648 | tf_op jit(solution)/shard_map/pallas_call | solution.py:59
  2.0 2.2 %collective-permute-start.3 = (bf16[144,2048]{1,0:T(8,128)(2,1)S(1)}, bf16[144,2048]{1,0:T(8,128)(2,1)S(1)}, u32[]{:S(2)}, u32[]{:S(2)}) collective-permute-start(bf16[144,2048]{1,0:T(8,128)(2,1)S(1)} %shard_map.80), channel_id=1, source_target_pairs={{0,32},{1,129},{16,48},{17,145},{32,0},{33,161},{48,16},{49,177},{... | collective-permute-start | bytes 1769480 | tf_op jit(solution)/shard_map/ppermute | solution.py:30
  4.2 0.2 shard_map.81
  4.4 1.5 %collective-permute-start.4 = (bf16[144,2048]{1,0:T(8,128)(2,1)S(1)}, bf16[144,2048]{1,0:T(8,128)(2,1)S(1)}, u32[]{:S(2)}, u32[]{:S(2)}) collective-permute-start(bf16[144,2048]{1,0:T(8,128)(2,1)S(1)} %shard_map.81), channel_id=1, source_target_pairs={{0,16},{1,65},{16,0},{17,81},{32,48},{33,97},{48,32},{49,113},{64,... | collective-permute-start | bytes 1769480 | tf_op jit(solution)/shard_map/ppermute | solution.py:30
  5.9 0.2 shard_map.82
  6.1 0.6 collective-permute-start.5
  6.8 0.1 shard_map.76
  6.8 2.2 %collective-permute-start = (bf16[48,2048]{1,0:T(8,128)(2,1)S(1)}, bf16[48,2048]{1,0:T(8,128)(2,1)S(1)}, u32[]{:S(2)}, u32[]{:S(2)}) collective-permute-start(bf16[48,2048]{1,0:T(8,128)(2,1)S(1)} %shard_map.76), channel_id=1, source_target_pairs={{0,32},{1,129},{16,48},{17,145},{32,0},{33,161},{48,16},{49,177},{... | collective-permute-start | bytes 589832 | tf_op jit(solution)/shard_map/ppermute | solution.py:30
  9.0 0.1 shard_map.77
  9.1 1.5 %collective-permute-start.1 = (bf16[48,2048]{1,0:T(8,128)(2,1)S(1)}, bf16[48,2048]{1,0:T(8,128)(2,1)S(1)}, u32[]{:S(2)}, u32[]{:S(2)}) collective-permute-start(bf16[48,2048]{1,0:T(8,128)(2,1)S(1)} %shard_map.77), channel_id=1, source_target_pairs={{0,16},{1,65},{16,0},{17,81},{32,48},{33,97},{48,32},{49,113},{64,... | collective-permute-start | bytes 589832 | tf_op jit(solution)/shard_map/ppermute | solution.py:30
  10.6 0.2 shard_map.79
  10.8 0.1 shard_map.78
  10.9 2.7 %collective-permute-done.3 = bf16[144,2048]{1,0:T(8,128)(2,1)S(1)} collective-permute-done((bf16[144,2048]{1,0:T(8,128)(2,1)S(1)}, bf16[144,2048]{1,0:T(8,128)(2,1)S(1)}, u32[]{:S(2)}, u32[]{:S(2)}) %collective-permute-start.3) | collective-permute-done | bytes 589856 | tf_op jit(solution)/shard_map/ppermute | solution.py:30
  13.6 1.5 %collective-permute-start.2 = (bf16[48,2048]{1,0:T(8,128)(2,1)S(1)}, bf16[48,2048]{1,0:T(8,128)(2,1)S(1)}, u32[]{:S(2)}, u32[]{:S(2)}) collective-permute-start(bf16[48,2048]{1,0:T(8,128)(2,1)S(1)} %shard_map.78), channel_id=1, source_target_pairs={{0,48},{1,193},{16,32},{17,209},{32,16},{33,225},{48,0},{49,241},{... | collective-permute-start | bytes 589832 | tf_op jit(solution)/shard_map/ppermute | solution.py:30
  15.1 4.8 %collective-permute-done.4 = bf16[144,2048]{1,0:T(8,128)(2,1)S(1)} collective-permute-done((bf16[144,2048]{1,0:T(8,128)(2,1)S(1)}, bf16[144,2048]{1,0:T(8,128)(2,1)S(1)}, u32[]{:S(2)}, u32[]{:S(2)}) %collective-permute-start.4) | collective-permute-done | bytes 589856 | tf_op jit(solution)/shard_map/ppermute | solution.py:30
  19.9 0.4 add_convert_fusion
  20.3 3.3 %collective-permute-start.6 = (bf16[48,2048]{1,0:T(8,128)(2,1)S(1)}, bf16[48,2048]{1,0:T(8,128)(2,1)S(1)}, u32[]{:S(2)}, u32[]{:S(2)}) collective-permute-start(bf16[48,2048]{1,0:T(8,128)(2,1)S(1)} %get-tuple-element.12), channel_id=1, source_target_pairs={{0,128},{1,33},{16,144},{17,49},{32,160},{33,1},{48,176},{49,17},{... | collective-permute-start | bytes 589832 | tf_op jit(solution)/shard_map/ppermute | solution.py:30
  23.6 0.7 collective-permute-start.7
  24.3 0.8 collective-permute-start.8
  25.1 0.1 shard_map.75
  25.1 0.0 copy-start.1
  25.1 0.0 copy-start.2
  25.1 0.0 copy-start.3
  25.2 2.4 %collective-permute-done.6 = bf16[48,2048]{1,0:T(8,128)(2,1)S(1)} collective-permute-done((bf16[48,2048]{1,0:T(8,128)(2,1)S(1)}, bf16[48,2048]{1,0:T(8,128)(2,1)S(1)}, u32[]{:S(2)}, u32[]{:S(2)}) %collective-permute-start.6) | collective-permute-done | bytes 196640 | tf_op jit(solution)/shard_map/ppermute | solution.py:30
  27.6 2.4 %collective-permute-done.7 = bf16[48,2048]{1,0:T(8,128)(2,1)S(1)} collective-permute-done((bf16[48,2048]{1,0:T(8,128)(2,1)S(1)}, bf16[48,2048]{1,0:T(8,128)(2,1)S(1)}, u32[]{:S(2)}, u32[]{:S(2)}) %collective-permute-start.7) | collective-permute-done | bytes 196640 | tf_op jit(solution)/shard_map/ppermute | solution.py:30
  30.0 1.1 %collective-permute-done.8 = bf16[48,2048]{1,0:T(8,128)(2,1)S(1)} collective-permute-done((bf16[48,2048]{1,0:T(8,128)(2,1)S(1)}, bf16[48,2048]{1,0:T(8,128)(2,1)S(1)}, u32[]{:S(2)}, u32[]{:S(2)}) %collective-permute-start.8) | collective-permute-done | bytes 196640 | tf_op jit(solution)/shard_map/ppermute | solution.py:30
  31.2 0.2 multiply_reduce_fusion
  31.4 16.0 %all_to_all.10 = f32[16,1,128]{2,1,0:T(1,128)S(1)} all-to-all(f32[16,1,128]{2,1,0:T(1,128)S(1)} %broadcast_in_dim.4), channel_id=1, replica_groups=mesh['dp_0'=4,'dp_1'=4,'shard_0'=8,'shard_1'=2] {'shard_0','shard_1'}, dimensions={0} | all-to-all | bytes 16384 | tf_op jit(solution)/shard_map/all_to_all | solution.py:110
  47.4 11.9 %all_to_all.11.squares = f32[16,1,128]{2,1,0:T(1,128)S(1)} all-to-all(f32[16,1,128]{2,1,0:T(1,128)S(1)} %broadcast_in_dim.5), channel_id=1, replica_groups=mesh['dp_0'=4,'dp_1'=4,'shard_0'=8,'shard_1'=2] {'dp_0','dp_1'}, dimensions={0} | all-to-all | bytes 16384 | tf_op jit(solution)/shard_map/all_to_all | solution.py:110
  59.4 0.7 owned_parameters.1
  60.0 1.3 %collective-permute-start.12 = (bf16[48,2048]{1,0:T(8,128)(2,1)S(1)}, bf16[48,2048]{1,0:T(8,128)(2,1)S(1)}, u32[]{:S(2)}, u32[]{:S(2)}) collective-permute-start(bf16[48,2048]{1,0:T(8,128)(2,1)S(1)} %owned_parameters.1), channel_id=1, source_target_pairs={{0,128},{1,33},{16,144},{17,49},{32,160},{33,1},{48,176},{49,17},{... | collective-permute-start | bytes 589832 | tf_op jit(solution)/shard_map/ppermute | solution.py:30
  61.3 2.1 %collective-permute-start.13 = (bf16[48,2048]{1,0:T(8,128)(2,1)S(1)}, bf16[48,2048]{1,0:T(8,128)(2,1)S(1)}, u32[]{:S(2)}, u32[]{:S(2)}) collective-permute-start(bf16[48,2048]{1,0:T(8,128)(2,1)S(1)} %owned_parameters.1), channel_id=1, source_target_pairs={{0,192},{1,49},{16,208},{17,33},{32,224},{33,17},{48,240},{49,1},{... | collective-permute-start | bytes 589832 | tf_op jit(solution)/shard_map/ppermute | solution.py:30
  63.4 0.2 collective-permute-start.9
  63.6 3.8 %collective-permute-done.12 = bf16[48,2048]{1,0:T(8,128)(2,1)S(1)} collective-permute-done((bf16[48,2048]{1,0:T(8,128)(2,1)S(1)}, bf16[48,2048]{1,0:T(8,128)(2,1)S(1)}, u32[]{:S(2)}, u32[]{:S(2)}) %collective-permute-start.12) | collective-permute-done | bytes 196640 | tf_op jit(solution)/shard_map/ppermute | solution.py:30
  67.4 2.0 %collective-permute-done.13 = bf16[48,2048]{1,0:T(8,128)(2,1)S(1)} collective-permute-done((bf16[48,2048]{1,0:T(8,128)(2,1)S(1)}, bf16[48,2048]{1,0:T(8,128)(2,1)S(1)}, u32[]{:S(2)}, u32[]{:S(2)}) %collective-permute-start.13) | collective-permute-done | bytes 196640 | tf_op jit(solution)/shard_map/ppermute | solution.py:30
  69.4 0.7 collective-permute-start.14
  70.1 2.1 %collective-permute-start.10 = (bf16[96,2048]{1,0:T(8,128)(2,1)S(1)}, bf16[96,2048]{1,0:T(8,128)(2,1)S(1)}, u32[]{:S(2)}, u32[]{:S(2)}) collective-permute-start(bf16[96,2048]{1,0:T(8,128)(2,1)S(1)} %pad_maximum_fusion.refs_0_), channel_id=1, source_target_pairs={{0,16},{1,65},{16,0},{17,81},{32,48},{33,97},{48,32},{49,113},{64,... | collective-permute-start | bytes 1179656 | tf_op jit(solution)/shard_map/ppermute | solution.py:30
  72.3 0.1 collective-permute-start.16
  72.4 1.5 %collective-permute-start.17 = (bf16[96,2048]{1,0:T(8,128)(2,1)S(1)}, bf16[96,2048]{1,0:T(8,128)(2,1)S(1)}, u32[]{:S(2)}, u32[]{:S(2)}) collective-permute-start(bf16[96,2048]{1,0:T(8,128)(2,1)S(1)} %pad_maximum_fusion.refs_0_), channel_id=1, source_target_pairs={{0,48},{1,193},{16,32},{17,209},{32,16},{33,225},{48,0},{49,241},{... | collective-permute-start | bytes 1179656 | tf_op jit(solution)/shard_map/ppermute | solution.py:30
  73.8 3.5 %collective-permute-done.14.refs_3_ = bf16[96,2048]{1,0:T(8,128)(2,1)S(1)} collective-permute-done((bf16[96,2048]{1,0:T(8,128)(2,1)S(1)}, bf16[96,2048]{1,0:T(8,128)(2,1)S(1)}, u32[]{:S(2)}, u32[]{:S(2)}) %collective-permute-start.14) | collective-permute-done | bytes 393248 | tf_op jit(solution)/shard_map/ppermute | solution.py:30
  77.3 2.7 %collective-permute-start.15 = (bf16[96,2048]{1,0:T(8,128)(2,1)S(1)}, bf16[96,2048]{1,0:T(8,128)(2,1)S(1)}, u32[]{:S(2)}, u32[]{:S(2)}) collective-permute-start(bf16[96,2048]{1,0:T(8,128)(2,1)S(1)} %collective-permute-done.14.refs_3_), channel_id=1, source_target_pairs={{0,16},{1,65},{16,0},{17,81},{32,48},{33,97},{48,32},{49,113},{64,... | collective-permute-start | bytes 1179656 | tf_op jit(solution)/shard_map/ppermute | solution.py:30
  80.0 0.6 collective-permute-start.11
  80.5 1.4 %new_state.1 = (f32[48,2048]{1,0:T(8,128)}, f32[48,2048]{1,0:T(8,128)}, f32[48,2048]{1,0:T(8,128)}) custom-call(f32[16,1,128]{2,1,0:T(1,128)S(1)} %all_to_all.11.squares, f32[48,2048]{1,0:T(8,128)S(1)} %get-tuple-element.11.summed, f32[48,2048]{1,0:T(8,128)S(1)} %copy-done.1, f32[48,2048]{1,0:T(8,128)S(1)} %copy-done.2, f32[48,2048]{1,0:T(8,128)S(1)} %copy-done.3), custom_call_target="tpu_custom_call" | custom-call | flops 2000000 | bytes 1769472 | tf_op jit(solution)/shard_map/new_state/pallas_call | solution.py:140
  82.0 1.2 %shard_map.83.refs_2_ = bf16[768,2048]{1,0:T(8,128)(2,1)} custom-call(bf16[96,2048]{1,0:T(8,128)(2,1)S(1)} %pad_maximum_fusion.refs_0_, bf16[96,2048]{1,0:T(8,128)(2,1)S(1)} %constant_dynamic-update-slice_fusion.refs_1_, bf16[96,2048]{1,0:T(8,128)(2,1)S(1)} %collective-permute-done.10.refs_2_, bf16[96,2048]{1,0:T(8,128)(2,1)S(1)} %collective-permute-done.14.refs_3_), custom_call_target="tpu_custom_call" | custom-call | flops 2000000 | bytes 3145728 | tf_op jit(solution)/shard_map/pallas_call | solution.py:93
  83.2 0.9 %shard_map.84.refs_2_ = bf16[768,2048]{1,0:T(8,128)(2,1)} custom-call(bf16[96,2048]{1,0:T(8,128)(2,1)S(1)} %collective-permute-done.16.refs_0_, bf16[96,2048]{1,0:T(8,128)(2,1)S(1)} %collective-permute-done.17.refs_1_, bf16[768,2048]{1,0:T(8,128)(2,1)} %shard_map.83.refs_2_), custom_call_target="tpu_custom_call", output_to_operand_aliasing={{}: (2, {})} | custom-call | flops 2000000 | bytes 1572864 | tf_op jit(solution)/shard_map/pallas_call | solution.py:93
  84.1 2.3 %collective-permute-done.15.refs_1_ = bf16[96,2048]{1,0:T(8,128)(2,1)S(1)} collective-permute-done((bf16[96,2048]{1,0:T(8,128)(2,1)S(1)}, bf16[96,2048]{1,0:T(8,128)(2,1)S(1)}, u32[]{:S(2)}, u32[]{:S(2)}) %collective-permute-start.15) | collective-permute-done | bytes 393248 | tf_op jit(solution)/shard_map/ppermute | solution.py:30
  86.5 1.3 %collective-permute-done.11.refs_0_ = bf16[96,2048]{1,0:T(8,128)(2,1)S(1)} collective-permute-done((bf16[96,2048]{1,0:T(8,128)(2,1)S(1)}, bf16[96,2048]{1,0:T(8,128)(2,1)S(1)}, u32[]{:S(2)}, u32[]{:S(2)}) %collective-permute-start.11) | collective-permute-done | bytes 393248 | tf_op jit(solution)/shard_map/ppermute | solution.py:30
  87.7 0.9 %shard_map.85 = bf16[768,2048]{1,0:T(8,128)(2,1)} custom-call(bf16[96,2048]{1,0:T(8,128)(2,1)S(1)} %collective-permute-done.11.refs_0_, bf16[96,2048]{1,0:T(8,128)(2,1)S(1)} %collective-permute-done.15.refs_1_, bf16[768,2048]{1,0:T(8,128)(2,1)} %shard_map.84.refs_2_), custom_call_target="tpu_custom_call", output_to_operand_aliasing={{}: (2, {})} | custom-call | flops 2000000 | bytes 1572864 | tf_op jit(solution)/shard_map/pallas_call | solution.py:93
  (21 shorter events, 0.2 us)
Async XLA Ops:
  0.6 3.6 %copy-start = (bf16[1,768,2048]{2,1,0:T(8,128)(2,1)S(1)}, bf16[1,768,2048]{2,1,0:T(8,128)(2,1)}, u32[]{:S(2)}) copy-start(bf16[1,768,2048]{2,1,0:T(8,128)(2,1)} %source.15) | copy-start | bytes 9437188
  2.0 11.6 %collective-permute-start.3 = (bf16[144,2048]{1,0:T(8,128)(2,1)S(1)}, bf16[144,2048]{1,0:T(8,128)(2,1)S(1)}, u32[]{:S(2)}, u32[]{:S(2)}) collective-permute-start(bf16[144,2048]{1,0:T(8,128)(2,1)S(1)} %shard_map.80), channel_id=1, source_target_pairs={{0,32},{1,129},{16,48},{17,145},{32,0},{33,161},{48,16},{49,177},{... | collective-permute-start | bytes 1769480 | tf_op jit(solution)/shard_map/ppermute | solution.py:30
  4.4 15.4 %collective-permute-start.4 = (bf16[144,2048]{1,0:T(8,128)(2,1)S(1)}, bf16[144,2048]{1,0:T(8,128)(2,1)S(1)}, u32[]{:S(2)}, u32[]{:S(2)}) collective-permute-start(bf16[144,2048]{1,0:T(8,128)(2,1)S(1)} %shard_map.81), channel_id=1, source_target_pairs={{0,16},{1,65},{16,0},{17,81},{32,48},{33,97},{48,32},{49,113},{64,... | collective-permute-start | bytes 1769480 | tf_op jit(solution)/shard_map/ppermute | solution.py:30
  6.1 13.7 %collective-permute-start.5 = (bf16[144,2048]{1,0:T(8,128)(2,1)S(1)}, bf16[144,2048]{1,0:T(8,128)(2,1)S(1)}, u32[]{:S(2)}, u32[]{:S(2)}) collective-permute-start(bf16[144,2048]{1,0:T(8,128)(2,1)S(1)} %shard_map.82), channel_id=1, source_target_pairs={{0,48},{1,193},{16,32},{17,209},{32,16},{33,225},{48,0},{49,241},{... | collective-permute-start | bytes 1769480 | tf_op jit(solution)/shard_map/ppermute | solution.py:30
  6.8 17.5 %collective-permute-start = (bf16[48,2048]{1,0:T(8,128)(2,1)S(1)}, bf16[48,2048]{1,0:T(8,128)(2,1)S(1)}, u32[]{:S(2)}, u32[]{:S(2)}) collective-permute-start(bf16[48,2048]{1,0:T(8,128)(2,1)S(1)} %shard_map.76), channel_id=1, source_target_pairs={{0,32},{1,129},{16,48},{17,145},{32,0},{33,161},{48,16},{49,177},{... | collective-permute-start | bytes 589832 | tf_op jit(solution)/shard_map/ppermute | solution.py:30
  9.1 16.1 %collective-permute-start.1 = (bf16[48,2048]{1,0:T(8,128)(2,1)S(1)}, bf16[48,2048]{1,0:T(8,128)(2,1)S(1)}, u32[]{:S(2)}, u32[]{:S(2)}) collective-permute-start(bf16[48,2048]{1,0:T(8,128)(2,1)S(1)} %shard_map.77), channel_id=1, source_target_pairs={{0,16},{1,65},{16,0},{17,81},{32,48},{33,97},{48,32},{49,113},{64,... | collective-permute-start | bytes 589832 | tf_op jit(solution)/shard_map/ppermute | solution.py:30
  13.6 11.6 %collective-permute-start.2 = (bf16[48,2048]{1,0:T(8,128)(2,1)S(1)}, bf16[48,2048]{1,0:T(8,128)(2,1)S(1)}, u32[]{:S(2)}, u32[]{:S(2)}) collective-permute-start(bf16[48,2048]{1,0:T(8,128)(2,1)S(1)} %shard_map.78), channel_id=1, source_target_pairs={{0,48},{1,193},{16,32},{17,209},{32,16},{33,225},{48,0},{49,241},{... | collective-permute-start | bytes 589832 | tf_op jit(solution)/shard_map/ppermute | solution.py:30
  20.3 7.3 %collective-permute-start.6 = (bf16[48,2048]{1,0:T(8,128)(2,1)S(1)}, bf16[48,2048]{1,0:T(8,128)(2,1)S(1)}, u32[]{:S(2)}, u32[]{:S(2)}) collective-permute-start(bf16[48,2048]{1,0:T(8,128)(2,1)S(1)} %get-tuple-element.12), channel_id=1, source_target_pairs={{0,128},{1,33},{16,144},{17,49},{32,160},{33,1},{48,176},{49,17},{... | collective-permute-start | bytes 589832 | tf_op jit(solution)/shard_map/ppermute | solution.py:30
  23.6 6.4 %collective-permute-start.7 = (bf16[48,2048]{1,0:T(8,128)(2,1)S(1)}, bf16[48,2048]{1,0:T(8,128)(2,1)S(1)}, u32[]{:S(2)}, u32[]{:S(2)}) collective-permute-start(bf16[48,2048]{1,0:T(8,128)(2,1)S(1)} %get-tuple-element.14), channel_id=1, source_target_pairs={{0,64},{1,17},{16,80},{17,1},{32,96},{33,49},{48,112},{49,33},{64,... | collective-permute-start | bytes 589832 | tf_op jit(solution)/shard_map/ppermute | solution.py:30
  24.3 6.9 %collective-permute-start.8 = (bf16[48,2048]{1,0:T(8,128)(2,1)S(1)}, bf16[48,2048]{1,0:T(8,128)(2,1)S(1)}, u32[]{:S(2)}, u32[]{:S(2)}) collective-permute-start(bf16[48,2048]{1,0:T(8,128)(2,1)S(1)} %get-tuple-element.13), channel_id=1, source_target_pairs={{0,192},{1,49},{16,208},{17,33},{32,224},{33,17},{48,240},{49,1},{... | collective-permute-start | bytes 589832 | tf_op jit(solution)/shard_map/ppermute | solution.py:30
  25.1 34.2 %copy-start.1 = (f32[48,2048]{1,0:T(8,128)S(1)}, f32[48,2048]{1,0:T(8,128)}, u32[]{:S(2)}) copy-start(f32[48,2048]{1,0:T(8,128)} %master.3) | copy-start | bytes 1179652
  25.1 34.2 %copy-start.2 = (f32[48,2048]{1,0:T(8,128)S(1)}, f32[48,2048]{1,0:T(8,128)}, u32[]{:S(2)}) copy-start(f32[48,2048]{1,0:T(8,128)} %first.3) | copy-start | bytes 1179652
  25.1 34.2 %copy-start.3 = (f32[48,2048]{1,0:T(8,128)S(1)}, f32[48,2048]{1,0:T(8,128)}, u32[]{:S(2)}) copy-start(f32[48,2048]{1,0:T(8,128)} %second.3) | copy-start | bytes 1179652
  60.0 7.4 %collective-permute-start.12 = (bf16[48,2048]{1,0:T(8,128)(2,1)S(1)}, bf16[48,2048]{1,0:T(8,128)(2,1)S(1)}, u32[]{:S(2)}, u32[]{:S(2)}) collective-permute-start(bf16[48,2048]{1,0:T(8,128)(2,1)S(1)} %owned_parameters.1), channel_id=1, source_target_pairs={{0,128},{1,33},{16,144},{17,49},{32,160},{33,1},{48,176},{49,17},{... | collective-permute-start | bytes 589832 | tf_op jit(solution)/shard_map/ppermute | solution.py:30
  61.3 8.1 %collective-permute-start.13 = (bf16[48,2048]{1,0:T(8,128)(2,1)S(1)}, bf16[48,2048]{1,0:T(8,128)(2,1)S(1)}, u32[]{:S(2)}, u32[]{:S(2)}) collective-permute-start(bf16[48,2048]{1,0:T(8,128)(2,1)S(1)} %owned_parameters.1), channel_id=1, source_target_pairs={{0,192},{1,49},{16,208},{17,33},{32,224},{33,17},{48,240},{49,1},{... | collective-permute-start | bytes 589832 | tf_op jit(solution)/shard_map/ppermute | solution.py:30
  63.4 6.7 %collective-permute-start.9 = (bf16[48,2048]{1,0:T(8,128)(2,1)S(1)}, bf16[48,2048]{1,0:T(8,128)(2,1)S(1)}, u32[]{:S(2)}, u32[]{:S(2)}) collective-permute-start(bf16[48,2048]{1,0:T(8,128)(2,1)S(1)} %owned_parameters.1), channel_id=1, source_target_pairs={{0,64},{1,17},{16,80},{17,1},{32,96},{33,49},{48,112},{49,33},{64,... | collective-permute-start | bytes 589832 | tf_op jit(solution)/shard_map/ppermute | solution.py:30
  69.4 7.9 %collective-permute-start.14 = (bf16[96,2048]{1,0:T(8,128)(2,1)S(1)}, bf16[96,2048]{1,0:T(8,128)(2,1)S(1)}, u32[]{:S(2)}, u32[]{:S(2)}) collective-permute-start(bf16[96,2048]{1,0:T(8,128)(2,1)S(1)} %constant_dynamic-update-slice_fusion.refs_1_), channel_id=1, source_target_pairs={{0,48},{1,193},{16,32},{17,209},{32,16},{33,225},{48,0},{49,241},{... | collective-permute-start | bytes 1179656 | tf_op jit(solution)/shard_map/ppermute | solution.py:30
  70.1 9.8 %collective-permute-start.10 = (bf16[96,2048]{1,0:T(8,128)(2,1)S(1)}, bf16[96,2048]{1,0:T(8,128)(2,1)S(1)}, u32[]{:S(2)}, u32[]{:S(2)}) collective-permute-start(bf16[96,2048]{1,0:T(8,128)(2,1)S(1)} %pad_maximum_fusion.refs_0_), channel_id=1, source_target_pairs={{0,16},{1,65},{16,0},{17,81},{32,48},{33,97},{48,32},{49,113},{64,... | collective-permute-start | bytes 1179656 | tf_op jit(solution)/shard_map/ppermute | solution.py:30
  72.3 10.9 %collective-permute-start.16 = (bf16[96,2048]{1,0:T(8,128)(2,1)S(1)}, bf16[96,2048]{1,0:T(8,128)(2,1)S(1)}, u32[]{:S(2)}, u32[]{:S(2)}) collective-permute-start(bf16[96,2048]{1,0:T(8,128)(2,1)S(1)} %constant_dynamic-update-slice_fusion.refs_1_), channel_id=1, source_target_pairs={{0,16},{1,65},{16,0},{17,81},{32,48},{33,97},{48,32},{49,113},{64,... | collective-permute-start | bytes 1179656 | tf_op jit(solution)/shard_map/ppermute | solution.py:30
  72.4 10.8 %collective-permute-start.17 = (bf16[96,2048]{1,0:T(8,128)(2,1)S(1)}, bf16[96,2048]{1,0:T(8,128)(2,1)S(1)}, u32[]{:S(2)}, u32[]{:S(2)}) collective-permute-start(bf16[96,2048]{1,0:T(8,128)(2,1)S(1)} %pad_maximum_fusion.refs_0_), channel_id=1, source_target_pairs={{0,48},{1,193},{16,32},{17,209},{32,16},{33,225},{48,0},{49,241},{... | collective-permute-start | bytes 1179656 | tf_op jit(solution)/shard_map/ppermute | solution.py:30
  77.3 9.2 %collective-permute-start.15 = (bf16[96,2048]{1,0:T(8,128)(2,1)S(1)}, bf16[96,2048]{1,0:T(8,128)(2,1)S(1)}, u32[]{:S(2)}, u32[]{:S(2)}) collective-permute-start(bf16[96,2048]{1,0:T(8,128)(2,1)S(1)} %collective-permute-done.14.refs_3_), channel_id=1, source_target_pairs={{0,16},{1,65},{16,0},{17,81},{32,48},{33,97},{48,32},{49,113},{64,... | collective-permute-start | bytes 1179656 | tf_op jit(solution)/shard_map/ppermute | solution.py:30
  80.0 7.8 %collective-permute-start.11 = (bf16[96,2048]{1,0:T(8,128)(2,1)S(1)}, bf16[96,2048]{1,0:T(8,128)(2,1)S(1)}, u32[]{:S(2)}, u32[]{:S(2)}) collective-permute-start(bf16[96,2048]{1,0:T(8,128)(2,1)S(1)} %collective-permute-done.10.refs_2_), channel_id=1, source_target_pairs={{0,48},{1,193},{16,32},{17,209},{32,16},{33,225},{48,0},{49,241},{... | collective-permute-start | bytes 1179656 | tf_op jit(solution)/shard_map/ppermute | solution.py:30
